TPU v7x, 128 devices: a whole 4x4x4 slice. The times are simulated.
128 devices in a mesh: lon: 32 (over z, y_lo, x), ch: 4 (over y_hi, core).
Axes of the slice: x: 4, y: 4 (y_hi: 2, y_lo: 2; y = y_hi * 2 + y_lo), z: 4, core: 2. Of those that a mesh axis runs over, the one named last changes fastest.
Arguments:
- grid_inputs: bfloat16 [921600, 474], P('lon'), may hold values from -6 to 6
- embed_weight: bfloat16 [474, 512], replicated, may hold values from -0.25 to 0.25
- embed_bias: float32 [512], replicated, may hold values from -3 to 3
- mesh_latent: bfloat16 [20480, 512], P('lon', 'ch'), may hold values from -6 to 6
- edge_features: bfloat16 [4, 720896], P(None, 'lon'), may hold values from -6 to 6
- senders: int32 [720896], P('lon'), may hold values from 0 to 921599, as said below
- receivers: int32 [720896], P('lon'), may hold values from 0 to 20479, as said below
- sender_weight: bfloat16 [512, 512], P(None, 'ch'), may hold values from -0.25 to 0.25
- receiver_weight: bfloat16 [512, 512], P(None, 'ch'), may hold values from -0.25 to 0.25
- feature_weight: bfloat16 [4, 512], P(None, 'ch'), may hold values from -3 to 3
- hidden_bias: float32 [512], P('ch'), may hold values from -3 to 3
- message_weight: bfloat16 [512, 512], P('ch'), may hold values from -0.25 to 0.25
- message_bias: float32 [512], replicated, may hold values from -1.2 to 1.2
- norm_gain: float32 [512], P('ch'), may hold values from 0.5 to 1.5
- norm_shift: float32 [512], P('ch'), may hold values from -3 to 3
Outputs:
- mesh_out: bfloat16 [20480, 512], P('lon', 'ch')
Inputs may be any that keep to these rules, and one draw needn't show every extreme that they name: Edge e belongs to block b = e // 22528. Its sender is c * 640 + t with latitude row t and a column c that lies, counted around the closed circle of 1440 columns, at most 4 columns before or after the block's own columns b * 45 to b * 45 + 44; some block reaches 4 columns on both sides. Within each aligned run of min(2048, 22528) edges of a block, the senders' columns, counted from the block's first widened column, lie within 7 consecutive columns. `receivers`: the receiver of edge e lies among the mesh nodes b * 640 to b * 640 + 639 of its block b = e // 22528; a mesh node may receive no edge.
All inputs are finite; a program needn't handle non-finite values.
Results may differ from a plain program's by a relative error of at most 0.0028.
Values may be sent and summed in bfloat16 or wider, within the bound.
No kernel may reach another device: no remote copies, remote signals or barrier semaphores. Data moves between devices by JAX's collectives and lax.ppermute only.
A program may use at most 128 MiB of HBM per device.

v0:
```python
import functools

import jax
import jax.numpy as jnp
from jax import lax
from jax.experimental import pallas as pl
from jax.experimental.pallas import tpu as pltpu
from jax.sharding import PartitionSpec as P


LAT = 640
HALO = 4
CHUNK = 512
SLOTS = 4
WINDOW = 7
PITCH = CHUNK + 8
BUFFERS = 8
LIMIT = 7

f32 = jnp.float32
bf16 = jnp.bfloat16


def silu(value):
    half = 0.5 * value
    return half + half * jnp.tanh(half)


def dot(left, right):
    return jnp.dot(left, right, preferred_element_type=f32)


def wide_row(ref, index):
    return ref[pl.ds(pl.multiple_of(index, 4), 4), :]


def chunk_of(tile):
    return jnp.concatenate([tile[j * PITCH : j * PITCH + CHUNK, :] for j in range(4)], axis=1)


def list_chunks(chunks, low_ref, high_ref, own_columns, outer, chunk_list):
    def step(i, counts):
        inner_count, outer_count = counts
        halo = (low_ref[i] < HALO) | (high_ref[i] >= HALO + own_columns)
        early = jnp.logical_not(halo) & (inner_count < LIMIT)
        count = outer_count if outer else inner_count

        @pl.when(jnp.logical_not(early) if outer else early)
        def _():
            chunk_list[count] = i

        return inner_count + jnp.where(early, 1, 0), outer_count + jnp.where(early, 0, 1)

    return lax.fori_loop(0, chunks, step, (jnp.int32(0), jnp.int32(0)))[1 if outer else 0]


def list_columns(count, first_chunk, low_ref, high_ref, chunk_list, column_list, offset_list):
    slot0 = lax.shift_right_logical(first_chunk, 2)
    total = jnp.int32(0)
    seg_first = jnp.int32(1000)
    seg_last = jnp.int32(-1)
    seg_start = jnp.int32(0)
    for slot in range(SLOTS):

        def step(t, carry):
            low, high = carry
            i = chunk_list[t]
            here = lax.shift_right_logical(first_chunk + i, 2) == slot0 + slot
            return (
                jnp.where(here, jnp.minimum(low, low_ref[i]), low),
                jnp.where(here, jnp.maximum(high, high_ref[i]), high),
            )

        low, high = lax.fori_loop(0, count, step, (jnp.int32(1000), jnp.int32(-1)))
        has = high >= 0
        joins = has & (low >= seg_first) & (low <= seg_last + 1)
        begin = jnp.where(joins, seg_last + 1, low)
        fresh = jnp.where(has, jnp.maximum(high - begin + 1, 0), 0)
        base = total

        def put(j, carry):
            column_list[base + j] = begin + j
            return carry

        lax.fori_loop(0, fresh, put, 0)
        opens = has & jnp.logical_not(joins)
        seg_start = jnp.where(opens, total, seg_start)
        seg_first = jnp.where(opens, low, seg_first)
        seg_last = jnp.where(opens, high, jnp.maximum(seg_last, high))
        total = total + fresh
        offset_list[slot] = (seg_start - seg_first) * (LAT * 4)
    return total


def block_kernel(outer, chunks, own_columns, channels, nodes, *refs):
    place, low_ref, high_ref, grid = refs[:4]
    refs = refs[4:]
    if outer:
        low_own, low_swap, high_own, high_swap = refs[:4]
        refs = refs[4:]
    points, embed_in, embed_bias, ids, features = refs[:5]
    bundles = refs[5:9]
    meshes = refs[9:13]
    refs = refs[13:]
    if outer:
        messages = refs[:4]
        refs = refs[4:]
        message_bias, first_totals, first_tally, *parts = refs[:7]
        totals, tally = refs[-2:]
        refs = refs[7:-2]
    else:
        totals, tally = refs[:2]
        refs = refs[2:]
    (table, columns, sent, got, inputs, rows, embed_weight, send_weight, recv_weight,
     message_weight, mesh, extras, placed, placed_s, recv_s, chunk_list, column_list, offset_list,
     in_sems, sems) = refs
    k = place[0]
    core = lax.bitwise_and(k, 1)
    first_chunk = k * chunks
    count = list_chunks(chunks, low_ref, high_ref, own_columns, outer, chunk_list)
    total = list_columns(
        count, first_chunk, low_ref, high_ref, chunk_list, column_list, offset_list
    )

    copies = []
    for j in range(4):
        lanes = pl.ds(j * 128, 128)
        copies.append((bundles[j].at[pl.ds(0, 512)], send_weight.at[:, lanes]))
        copies.append((bundles[j].at[pl.ds(512, 512)], recv_weight.at[:, lanes]))
        copies.append((bundles[j].at[pl.ds(1024, 16)], extras.at[j]))
        at = pl.multiple_of(jnp.bitwise_xor(k, j) * 128, 128)
        copies.append((meshes[j], mesh.at[:, pl.ds(at, 128)]))
    copies = [pltpu.make_async_copy(a, b, sems.at[n]) for n, (a, b) in enumerate(copies)]
    late = []
    if outer:
        for j in range(4):
            late.append(
                pltpu.make_async_copy(
                    messages[j], message_weight.at[pl.ds(j * 128, 128)], sems.at[16 + j]
                )
            )
        for copy in late:
            copy.start()
        totals[...] = first_totals[...]
        tally[...] = first_tally[...]
    else:
        totals[...] = jnp.zeros_like(totals)
        tally[...] = jnp.zeros_like(tally)

    def fetch(source, column, slot):
        start = pl.multiple_of(column * LAT, 128)
        pltpu.make_async_copy(
            source.at[:, pl.ds(start, LAT)], columns.at[slot], in_sems.at[slot]
        ).start()

    def start_column(i):
        column = column_list[i]
        slot = lax.rem(i, BUFFERS)
        if not outer:
            fetch(grid, column - HALO, slot)
            return
        inside = (column >= HALO) & (column < HALO + own_columns)

        @pl.when(inside)
        def _():
            fetch(grid, column - HALO, slot)

        for is_side, shift, direct, swapped in (
            (column < HALO, 0, low_own, low_swap),
            (column >= HALO + own_columns, HALO + own_columns, high_own, high_swap),
        ):
            place_in = column - shift
            half = lax.shift_right_arithmetic(place_in, 1)
            within = lax.bitwise_and(place_in, 1)

            @pl.when(is_side & (half == core))
            def _():
                fetch(direct, within, slot)

            @pl.when(is_side & (half != core))
            def _():
                fetch(swapped, within, slot)

    def turn(i, carry):
        slot = lax.rem(i, BUFFERS)

        @pl.when(i + BUFFERS - 1 < total)
        def _():
            start_column(i + BUFFERS - 1)

        pltpu.make_async_copy(
            grid.at[:, pl.ds(0, LAT)], columns.at[slot], in_sems.at[slot]
        ).wait()
        source = columns.at[slot]
        for l in range(LAT // 128):
            lanes = pl.ds(l * 128, 128)
            for j in range(4):
                top = min(channels, (j + 1) * 128)
                block = source[j * 128 : top, lanes]
                if top < (j + 1) * 128:
                    block = jnp.pad(block, ((0, (j + 1) * 128 - top), (0, 0)))
                row = pl.multiple_of((i * LAT + l * 128) * 4, 8)
                table[pl.ds(row + j, 128, stride=4), :] = block.T.astype(f32)
        return carry

    def indices(ref, t):
        return ref.at[pl.ds(pl.multiple_of(chunk_list[t] * 4, 4), 4)]

    def gather(source, picks, target):
        for e in range(CHUNK):
            target[pl.ds(e, 4, stride=PITCH), :] = wide_row(source, picks[e // 128, e % 128])

    index_copies = [
        pltpu.make_async_copy(placed, placed_s, sems.at[30]),
        pltpu.make_async_copy(ids, recv_s, sems.at[31]),
    ]

    @pl.when(count > 0)
    def _():
        for b in range(BUFFERS - 1):

            @pl.when(b < total)
            def _():
                start_column(b)

        for i in range(chunks):
            slot = lax.shift_right_logical(first_chunk + i, 2) - lax.shift_right_logical(
                first_chunk, 2
            )
            placed[i * 4 : i * 4 + 4, :] = points[i * 4 : i * 4 + 4, :] + offset_list[slot]
        for copy in index_copies:
            copy.start()
        for copy in copies:
            copy.start()
        embed_weight[464:512, :] = jnp.zeros((48, 512), bf16)
        embed_weight[0:channels, :] = embed_in[...]
        lax.fori_loop(0, total, turn, 0)
        for copy in copies + index_copies:
            copy.wait()
        bias = jnp.concatenate(
            [
                sum(extras[j, 4 + r : 5 + r, :].astype(f32) for r in range(3))
                for j in range(4)
            ],
            axis=1,
        )
        terms = dot(mesh[...], recv_weight[...]) + bias
        for j in range(4):
            rows[pl.ds(j, nodes, stride=4), :] = terms[:, j * 128 : (j + 1) * 128]
        gather(table, indices(placed_s, 0), sent)
        features_by = jnp.concatenate([extras[j, 0:4, :] for j in range(4)], axis=1)

        def work(t, carry):
            i = chunk_list[t]
            inputs[...] = chunk_of(sent).astype(bf16)
            gather(rows, indices(recv_s, t), got)
            latent = silu(dot(inputs[...], embed_weight[...]) + embed_bias[...]).astype(bf16)
            before = (
                dot(latent, send_weight[...])
                + chunk_of(got)
                + lax.dot_general(
                    features[first_chunk + i], features_by, (((0,), (0,)), ((), ())),
                    preferred_element_type=f32,
                )
            )
            hidden = silu(before).astype(bf16)
            node = lax.broadcasted_iota(jnp.int32, (nodes, 128), 0) * 4
            hots = [
                jnp.where(node == ids[pl.ds(i * 4 + q, 1), :], 1.0, 0.0) for q in range(4)
            ]
            hot = jnp.concatenate([value.astype(bf16) for value in hots], axis=1)
            gather(table, indices(placed_s, jnp.minimum(t + 1, count - 1)), sent)
            totals[...] += dot(hot, hidden)
            tally[...] += (hots[0] + hots[1]) + (hots[2] + hots[3])
            return carry

        lax.fori_loop(0, count, work, 0)

    if not outer:
        return
    counts = jnp.sum(tally[...], axis=1, keepdims=True)
    whole = totals[...]
    upper = whole.astype(bf16)
    lower = (whole - upper.astype(f32)).astype(bf16)
    for copy in late:
        copy.wait()
    totals[...] = (
        dot(upper, message_weight[...])
        + dot(lower, message_weight[...])
        + counts * message_bias[...]
    )
    for r in range(2):
        mine = pl.multiple_of(jnp.bitwise_xor(k, 2 * r) * 128, 128)
        theirs = pl.multiple_of(jnp.bitwise_xor(k, 2 * r + 1) * 128, 128)
        parts[r][...] = totals[:, pl.ds(mine, 128)]
        parts[2 + r][...] = totals[:, pl.ds(theirs, 128)]


def weights_kernel(feature_weight, hidden_bias, sender_weight, receiver_weight, bundle):
    bundle[0:512, :] = sender_weight[...]
    bundle[512:1024, :] = receiver_weight[...]
    bias = hidden_bias[...]
    upper = bias.astype(bf16)
    middle = (bias - upper.astype(f32)).astype(bf16)
    lower = (bias - upper.astype(f32) - middle.astype(f32)).astype(bf16)
    bundle[1024:1040, :] = jnp.concatenate(
        [feature_weight[...].astype(f32)]
        + [value.astype(f32) for value in (upper, middle, lower)]
        + [jnp.zeros((9, bias.shape[1]), f32)],
        axis=0,
    ).astype(bf16)


def pack_kernel(chunks, points_own, all_points, nodes, lon_ref, place, senders, receivers, grid,
                points, ids, low_ref, high_ref, low_half, high_half, sems):
    lon = lon_ref[0]
    k = place[0]
    half = HALO * LAT // 2
    side = lax.bitwise_and(k, 1) * half
    low_at = pl.multiple_of(points_own - 2 * half + side, 128)
    copies = [
        pltpu.make_async_copy(grid.at[:, pl.ds(low_at, half)], low_half, sems.at[0]),
        pltpu.make_async_copy(
            grid.at[:, pl.ds(pl.multiple_of(side, 128), half)], high_half, sems.at[1]
        ),
    ]
    for copy in copies:
        copy.start()
    for i in range(chunks):
        rows = pl.ds(pl.multiple_of((k * chunks + i) * 4, 4), 4)
        point = senders[rows, :] - lon * points_own + HALO * LAT
        point = jnp.where(point < 0, point + all_points, point)
        point = jnp.where(point >= all_points, point - all_points, point)
        points[i * 4 : i * 4 + 4, :] = point * 4
        ids[i * 4 : i * 4 + 4, :] = (receivers[rows, :] - lon * nodes) * 4
        for ref, end in ((low_ref, jnp.min(point)), (high_ref, jnp.max(point))):
            ref[i] = lax.shift_right_logical(lax.shift_right_logical(end, 7) * 13108, 16)
    for copy in copies:
        copy.wait()


def weights_call(share, operands):
    return pl.pallas_call(
        weights_kernel,
        out_shape=jax.ShapeDtypeStruct((1040, share), bf16),
        in_specs=[VMEM] * 4,
        out_specs=VMEM,
        name="weights",
    )(*operands)


def pack_call(chunks, points_own, all_points, channels, nodes, operands):
    half = HALO * LAT // 2
    index = jax.ShapeDtypeStruct((chunks * 4, 128), jnp.int32)
    ends = jax.ShapeDtypeStruct((chunks,), jnp.int32)
    side = jax.ShapeDtypeStruct((channels, half), bf16)
    return pl.pallas_call(
        functools.partial(pack_kernel, chunks, points_own, all_points, nodes),
        out_shape=(index, index, ends, ends, side, side),
        in_specs=[SMEM] * 2 + [VMEM] * 2 + [ANY],
        out_specs=(VMEM, VMEM, SMEM, SMEM, VMEM, VMEM),
        scratch_shapes=[pltpu.SemaphoreType.DMA((2,))],
        name="pack",
    )(*operands)


VMEM = pl.BlockSpec(memory_space=pltpu.VMEM)
SMEM = pl.BlockSpec(memory_space=pltpu.SMEM)
ANY = pl.BlockSpec(memory_space=pl.ANY)


def block_call(outer, chunks, own_columns, channels, nodes, operands):
    width = 512
    part = jax.ShapeDtypeStruct((nodes, 128), f32)
    sums = (
        jax.ShapeDtypeStruct((nodes, width), f32),
        jax.ShapeDtypeStruct((nodes, 128), f32),
    )
    specs = [SMEM] * 3 + [ANY] * (5 if outer else 1) + [VMEM] * 5 + [ANY] * 8
    if outer:
        specs = specs + [ANY] * 4 + [VMEM] * 3
    slots = SLOTS * WINDOW
    edges = chunks * CHUNK
    square = pltpu.VMEM((width, width), bf16)
    return pl.pallas_call(
        functools.partial(block_kernel, outer, chunks, own_columns, channels, nodes),
        out_shape=(part,) * 4 if outer else sums,
        in_specs=specs,
        out_specs=(VMEM,) * (4 if outer else 2),
        scratch_shapes=[
            pltpu.VMEM((slots * LAT * 4, 128), f32),
            pltpu.VMEM((BUFFERS, channels, LAT), bf16),
            pltpu.VMEM((4 * PITCH, 128), f32),
            pltpu.VMEM((4 * PITCH, 128), f32),
            pltpu.VMEM((CHUNK, width), bf16),
            pltpu.VMEM((nodes * 4, 128), f32),
            square,
            square,
            square,
            square,
            pltpu.VMEM((nodes, width), bf16),
            pltpu.VMEM((4, 16, 128), bf16),
            pltpu.VMEM((chunks * 4, 128), jnp.int32),
            pltpu.SMEM((chunks * 4, 128), jnp.int32),
            pltpu.SMEM((chunks * 4, 128), jnp.int32),
            pltpu.SMEM((16,), jnp.int32),
            pltpu.SMEM((32,), jnp.int32),
            pltpu.SMEM((8,), jnp.int32),
            pltpu.SemaphoreType.DMA((BUFFERS,)),
            pltpu.SemaphoreType.DMA((32,)),
        ]
        + ([pltpu.VMEM(value.shape, f32) for value in sums] if outer else []),
        compiler_params=pltpu.CompilerParams(vmem_limit_bytes=60 * 2**20),
        cost_estimate=pl.CostEstimate(
            flops=2 * edges * width * (2 * width + nodes),
            bytes_accessed=2 * edges * width,
            transcendentals=2 * edges * width,
        ),
        name="block_outer" if outer else "block_inner",
    )(*operands)


def encoder(
    grid_inputs,
    embed_weight,
    embed_bias,
    mesh_latent,
    edge_features,
    senders,
    receivers,
    sender_weight,
    receiver_weight,
    feature_weight,
    hidden_bias,
    message_weight,
    message_bias,
    norm_gain,
    norm_shift,
):
    lon_count = lax.axis_size("lon")
    ch_count = lax.axis_size("ch")
    lon_place = lax.axis_index("lon")
    ch_place = lax.axis_index("ch")
    place = ch_place[None].astype(jnp.int32)
    points_own, channels = grid_inputs.shape
    own_columns = points_own // LAT
    mesh_nodes = mesh_latent.shape[0]
    full_width = message_weight.shape[1]
    edge_count = senders.shape[0]
    all_chunks = edge_count // CHUNK
    chunks = all_chunks // ch_count

    swap = [(i, i ^ 1) for i in range(ch_count)]
    across = [(i, i ^ 2) for i in range(ch_count)]
    facing = [
        (lon * ch_count + ch, (lon ^ 4) * ch_count + (ch ^ 2))
        for lon in range(lon_count)
        for ch in range(ch_count)
    ]
    forward = [(i, (i + 1) % lon_count) for i in range(lon_count)]
    backward = [(target, source) for source, target in forward]

    flat = grid_inputs.T
    lon_scalar = lon_place[None].astype(jnp.int32)
    bundle = weights_call(
        message_weight.shape[0],
        [feature_weight, hidden_bias[None, :], sender_weight, receiver_weight],
    )
    bundle_far = lax.ppermute(bundle, ("lon", "ch"), facing)
    mesh_far = lax.ppermute(mesh_latent, "ch", across)
    points, ids, low_column, high_column, low_half, high_half = pack_call(
        chunks, points_own, points_own * lon_count, channels, mesh_nodes,
        [lon_scalar, place, senders.reshape(-1, 128), receivers.reshape(-1, 128), flat],
    )
    low_own = lax.ppermute(low_half, "lon", forward)
    high_own = lax.ppermute(high_half, "lon", backward)
    low_swap = lax.ppermute(low_own, "ch", swap)
    high_swap = lax.ppermute(high_own, "ch", swap)
    bundle_near = lax.ppermute(bundle, "ch", swap)
    bundle_last = lax.ppermute(bundle_far, "ch", swap)
    mesh_near = lax.ppermute(mesh_latent, "ch", swap)
    mesh_last = lax.ppermute(mesh_far, "ch", swap)
    message_far = lax.ppermute(message_weight, ("lon", "ch"), facing)
    message_near = lax.ppermute(message_weight, "ch", swap)
    message_last = lax.ppermute(message_far, "ch", swap)
    feature_blocks = jnp.transpose(
        edge_features.reshape(edge_features.shape[0], all_chunks, CHUNK), (1, 0, 2)
    )

    call = functools.partial(
        block_call, chunks=chunks, own_columns=own_columns, channels=channels, nodes=mesh_nodes
    )
    scalars = [place, low_column, high_column, flat]
    arrays = [
        points, embed_weight, embed_bias[None, :], ids, feature_blocks,
        bundle, bundle_near, bundle_far, bundle_last,
        mesh_latent, mesh_near, mesh_far, mesh_last,
    ]
    totals, tally = call(False, operands=scalars + arrays)
    keep_here, keep_far, send_here, send_far = call(
        True,
        operands=scalars
        + [low_own, low_swap, high_own, high_swap]
        + arrays
        + [message_weight, message_near, message_far, message_last]
        + [message_bias[None, :], totals, tally],
    )
    far = keep_far + lax.ppermute(send_far, "ch", swap)
    far = lax.ppermute(far.astype(bf16), "ch", across).astype(f32)
    node_share = keep_here + lax.ppermute(send_here, "ch", swap) + far
    first_sum, second = lax.psum(
        (
            jnp.sum(node_share, axis=1, keepdims=True),
            jnp.sum(jnp.square(node_share), axis=1, keepdims=True),
        ),
        "ch",
    )
    centre = first_sum / full_width
    spread = second / full_width - jnp.square(centre)
    normed = (node_share - centre) * lax.rsqrt(spread + 1.0)
    return (mesh_latent.astype(f32) + normed * norm_gain + norm_shift).astype(bf16)


def solution(mesh):
    return jax.shard_map(
        encoder,
        mesh=mesh,
        in_specs=(
            P("lon", None),
            P(),
            P(),
            P("lon", "ch"),
            P(None, "lon"),
            P("lon"),
            P("lon"),
            P(None, "ch"),
            P(None, "ch"),
            P(None, "ch"),
            P("ch"),
            P("ch", None),
            P(),
            P("ch"),
            P("ch"),
        ),
        out_specs=P("lon", "ch"),
        check_vma=False,
    )
```

profile of v0, /device:TPU:6, one launch (start us, length us, event | category | flops | bytes accessed | tf_op | source)
XLA Modules:
  0.0 106.6 jit_solution(5520728089221768540)
XLA Ops:
  0.0 0.0 copy-start.10
  0.0 0.0 copy-start.2
  0.0 4.1 %pack.1 = (s32[44,128]{1,0:T(8,128)}, s32[44,128]{1,0:T(8,128)}, s32[11]{0:T(128)}, s32[11]{0:T(128)}, bf16[474,1280]{1,0:T(8,128)(2,1)}, /*index=5*/bf16[474,1280]{1,0:T(8,128)(2,1)}) custom-call(s32[1]{0:T(128)} %bitcast.1.lon_ref, s32[1]{0:T(128)} %bitcast.place.refs_0_, s32[176,128]{1,0:T(8,128)} %bitcast.16, s32[176,128]{1,0:T(8,128)} %bitcast.17, ...), custom_call_target="tpu_custom_call" | custom-call | tf_op jit(solution)/shard_map/pack/pallas_call | solution.py:357
  4.1 1.6 %collective-permute-start = (bf16[474,1280]{1,0:T(8,128)(2,1)}, bf16[474,1280]{1,0:T(8,128)(2,1)S(1)}, u32[]{:S(2)}, u32[]{:S(2)}) collective-permute-start(bf16[474,1280]{1,0:T(8,128)(2,1)} %get-tuple-element.19), channel_id=1, source_target_pairs={{0,4},{4,8},{8,12},{12,16},{16,20},{20,24},{24,28},{28,32},{32,36}... | collective-permute-start | bytes 3640328 | tf_op jit(solution)/shard_map/ppermute | solution.py:475
  5.7 0.5 collective-permute-start.2
  6.2 1.8 %weights.1.refs_9_.refs_13_ = bf16[1040,128]{1,0:T(8,128)(2,1)} custom-call(bf16[4,128]{1,0:T(4,128)(2,1)} %feature_weight.1, f32[1,128]{1,0:T(1,128)} %bitcast.21, bf16[512,128]{1,0:T(8,128)(2,1)} %sender_weight.1, bf16[512,128]{1,0:T(8,128)(2,1)} %receiver_weight.1), custom_call_target="tpu_custom_call" | custom-call | tf_op jit(solution)/shard_map/weights/pallas_call | solution.py:343
  8.0 3.0 %collective-permute-start.5 = (bf16[1040,128]{1,0:T(8,128)(2,1)}, bf16[1040,128]{1,0:T(8,128)(2,1)S(1)}, u32[]{:S(2)}, u32[]{:S(2)}) collective-permute-start(bf16[1040,128]{1,0:T(8,128)(2,1)} %weights.1.refs_9_.refs_13_), channel_id=1, source_target_pairs={{0,18},{1,19},{2,16},{3,17},{4,22},{5,23},{6,20},{7,21},{8,26},{9,... | collective-permute-start | bytes 798728 | tf_op jit(solution)/shard_map/ppermute | solution.py:469
  11.0 0.0 copy-done.10
  11.0 0.2 collective-permute-start.11
  11.3 0.0 copy-done.2
  11.3 2.0 %collective-permute-start.8 = (bf16[640,128]{1,0:T(8,128)(2,1)S(1)}, bf16[640,128]{1,0:T(8,128)(2,1)S(1)}, u32[]{:S(2)}, u32[]{:S(2)}) collective-permute-start(bf16[640,128]{1,0:T(8,128)(2,1)S(1)} %copy-done.2), channel_id=1, source_target_pairs={{0,2},{1,3},{2,0},{3,1},{4,6},{5,7},{6,4},{7,5},{8,10},{9,11},{10,... | collective-permute-start | bytes 491528 | tf_op jit(solution)/shard_map/ppermute | solution.py:470
  13.2 7.5 %collective-permute-done.11.refs_23_ = bf16[128,512]{1,0:T(8,128)(2,1)S(1)} collective-permute-done((bf16[128,512]{1,0:T(8,128)(2,1)S(1)}, bf16[128,512]{1,0:T(8,128)(2,1)S(1)}, u32[]{:S(2)}, u32[]{:S(2)}) %collective-permute-start.11) | collective-permute-done | bytes 131104 | tf_op jit(solution)/shard_map/ppermute | solution.py:483
  20.7 0.0 copy-start.11
  20.7 0.0 collective-permute-start.7
  20.7 12.4 %collective-permute-done.refs_4_ = bf16[474,1280]{1,0:T(8,128)(2,1)S(1)} collective-permute-done((bf16[474,1280]{1,0:T(8,128)(2,1)}, bf16[474,1280]{1,0:T(8,128)(2,1)S(1)}, u32[]{:S(2)}, u32[]{:S(2)}) %collective-permute-start) | collective-permute-done | bytes 1213472 | tf_op jit(solution)/shard_map/ppermute | solution.py:475
  33.2 0.0 copy-start
  33.2 0.0 collective-permute-start.1
  33.2 3.4 %collective-permute-done.2.refs_6_ = bf16[474,1280]{1,0:T(8,128)(2,1)S(1)} collective-permute-done((bf16[474,1280]{1,0:T(8,128)(2,1)}, bf16[474,1280]{1,0:T(8,128)(2,1)S(1)}, u32[]{:S(2)}, u32[]{:S(2)}) %collective-permute-start.2) | collective-permute-done | bytes 1213472 | tf_op jit(solution)/shard_map/ppermute | solution.py:476
  36.6 0.0 copy-start.1
  36.6 0.0 collective-permute-start.3
  36.6 7.7 %collective-permute-done.8.refs_15_.refs_19_ = bf16[640,128]{1,0:T(8,128)(2,1)S(1)} collective-permute-done((bf16[640,128]{1,0:T(8,128)(2,1)S(1)}, bf16[640,128]{1,0:T(8,128)(2,1)S(1)}, u32[]{:S(2)}, u32[]{:S(2)}) %collective-permute-start.8) | collective-permute-done | bytes 163872 | tf_op jit(solution)/shard_map/ppermute | solution.py:470
  44.3 0.0 copy-start.7
  44.3 0.0 collective-permute-start.4
  44.3 0.0 collective-permute-done.5.refs_11_.refs_15_
  44.3 0.0 copy-start.4
  44.3 0.5 collective-permute-start.6
  44.8 0.0 collective-permute-done.7.refs_14_.refs_18_
  44.8 0.1 collective-permute-start.9
  45.0 1.1 %collective-permute-done.4.refs_10_.refs_14_ = bf16[1040,128]{1,0:T(8,128)(2,1)S(1)} collective-permute-done((bf16[1040,128]{1,0:T(8,128)(2,1)}, bf16[1040,128]{1,0:T(8,128)(2,1)S(1)}, u32[]{:S(2)}, u32[]{:S(2)}) %collective-permute-start.4) | collective-permute-done | bytes 266272 | tf_op jit(solution)/shard_map/ppermute | solution.py:479
  46.1 0.1 collective-permute-start.10
  46.2 0.5 collective-permute-done.9.refs_16_.refs_20_
  46.7 0.1 collective-permute-start.12
  46.8 0.0 collective-permute-done.6.refs_12_.refs_16_
  46.8 0.0 copy-done.7
  46.8 0.0 copy-done.4
  46.8 0.0 copy-done.8
  46.9 0.0 copy-done.5
  46.9 0.5 copy-done.9
  47.4 0.2 copy-done.6
  47.6 21.7 %block_inner.1 = (f32[640,512]{1,0:T(8,128)}, f32[640,128]{1,0:T(8,128)}) custom-call(s32[1]{0:T(128)} %bitcast.place.refs_0_, s32[11]{0:T(128)} %get-tuple-element.17.refs_1_, s32[11]{0:T(128)} %get-tuple-element.18.refs_2_, bf16[474,28800]{1,0:T(8,128)(2,1)} %bitcast.12, s32[44,128]{1,0:T(8,128)} %get-tuple-element.21.refs_4_.refs_8_, ...), custom_call_target="tpu_custom_call" | custom-call | flops 9596567552 | bytes 5767168 | tf_op jit(solution)/shard_map/block_inner/pallas_call | solution.py:385
  69.3 0.0 copy-done.11
  69.3 0.0 copy-done
  69.3 0.0 copy-done.1
  69.3 0.0 collective-permute-done.10.refs_22_
  69.4 0.0 collective-permute-done.12.refs_24_
  69.4 0.0 collective-permute-done.1.refs_5_
  69.4 0.0 collective-permute-done.3.refs_7_
  69.4 16.9 %block_outer.1 = (f32[640,128]{1,0:T(8,128)}, f32[640,128]{1,0:T(8,128)}, f32[640,128]{1,0:T(8,128)}, f32[640,128]{1,0:T(8,128)}) custom-call(s32[1]{0:T(128)} %bitcast.place.refs_0_, s32[11]{0:T(128)} %get-tuple-element.17.refs_1_, s32[11]{0:T(128)} %get-tuple-element.18.refs_2_, bf16[474,28800]{1,0:T(8,128)(2,1)} %bitcast.13, bf16[474,1280]{1,0:T(8,128)(2,1)} %copy-done, ...), custom_call_target="tpu_custom_call" | custom-call | flops 9596567552 | bytes 5767168 | tf_op jit(solution)/shard_map/block_outer/pallas_call | solution.py:385
  86.3 0.0 copy-start.3
  86.3 0.0 copy-start.12
  86.3 0.0 copy-start.13
  86.3 0.2 collective-permute-start.14
  86.5 0.4 collective-permute-start.13
  86.9 1.3 %collective-permute-done.14 = f32[640,128]{1,0:T(8,128)S(1)} collective-permute-done((f32[640,128]{1,0:T(8,128)}, f32[640,128]{1,0:T(8,128)S(1)}, u32[]{:S(2)}, u32[]{:S(2)}) %collective-permute-start.14) | collective-permute-done | bytes 327712 | tf_op jit(solution)/shard_map/ppermute | solution.py:508
  88.2 1.0 add_convert_fusion.1
  89.3 0.9 collective-permute-start.15
  90.1 0.0 collective-permute-done.13
  90.1 7.0 %collective-permute-done.15 = bf16[640,128]{1,0:T(8,128)(2,1)S(1)} collective-permute-done((bf16[640,128]{1,0:T(8,128)(2,1)S(1)}, bf16[640,128]{1,0:T(8,128)(2,1)S(1)}, u32[]{:S(2)}, u32[]{:S(2)}) %collective-permute-start.15) | collective-permute-done | bytes 163872 | tf_op jit(solution)/shard_map/ppermute | solution.py:509
  97.1 1.2 %fusion = (f32[640]{0:T(1024)S(1)}, f32[640]{0:T(1024)S(1)}, f32[640,128]{1,0:T(8,128)S(1)}) fusion(bf16[640,128]{1,0:T(8,128)(2,1)S(1)} %collective-permute-done.15, f32[640,128]{1,0:T(8,128)} %get-tuple-element.25, f32[640,128]{1,0:T(8,128)S(1)} %collective-permute-done.13), kind=kLoop, calls=%fused_computation.6 | loop fusion | flops 490240 | bytes 1152000 | tf_op jit(solution)/shard_map/reduce_sum | solution.py:513
  98.4 7.2 %all-reduce = (f32[640,1]{0,1:T(1,128)S(1)}, f32[640,1]{0,1:T(1,128)S(1)}) all-reduce(f32[640,1]{0,1:T(1,128)S(1)} %broadcast_in_dim.28, f32[640,1]{0,1:T(1,128)S(1)} %broadcast_in_dim.29), channel_id=1, replica_groups=mesh['lon'=32,'ch'=4] {'ch'}, use_global_device_ids=true, to_apply=%region_1.0 | all-reduce | flops 1280 | bytes 10240 | tf_op jit(solution)/shard_map/psum | solution.py:511
  105.6 0.0 copy-done.3
  105.7 0.0 copy-done.12
  105.7 0.0 copy-done.13
  105.7 0.9 add_convert_fusion
  (7 shorter events, 0.0 us)
Async XLA Ops:
  0.0 11.0 %copy-start.10 = (bf16[128,512]{1,0:T(8,128)(2,1)S(1)}, bf16[128,512]{1,0:T(8,128)(2,1)}, u32[]{:S(2)}) copy-start(bf16[128,512]{1,0:T(8,128)(2,1)} %refs_21_.1) | copy-start | bytes 393220
  0.0 11.3 %copy-start.2 = (bf16[640,128]{1,0:T(8,128)(2,1)S(1)}, bf16[640,128]{1,0:T(8,128)(2,1)}, u32[]{:S(2)}) copy-start(bf16[640,128]{1,0:T(8,128)(2,1)} %refs_17_.1) | copy-start | bytes 491524
  4.1 29.0 %collective-permute-start = (bf16[474,1280]{1,0:T(8,128)(2,1)}, bf16[474,1280]{1,0:T(8,128)(2,1)S(1)}, u32[]{:S(2)}, u32[]{:S(2)}) collective-permute-start(bf16[474,1280]{1,0:T(8,128)(2,1)} %get-tuple-element.19), channel_id=1, source_target_pairs={{0,4},{4,8},{8,12},{12,16},{16,20},{20,24},{24,28},{28,32},{32,36}... | collective-permute-start | bytes 3640328 | tf_op jit(solution)/shard_map/ppermute | solution.py:475
  5.7 30.9 %collective-permute-start.2 = (bf16[474,1280]{1,0:T(8,128)(2,1)}, bf16[474,1280]{1,0:T(8,128)(2,1)S(1)}, u32[]{:S(2)}, u32[]{:S(2)}) collective-permute-start(bf16[474,1280]{1,0:T(8,128)(2,1)} %get-tuple-element.20), channel_id=1, source_target_pairs={{4,0},{8,4},{12,8},{16,12},{20,16},{24,20},{28,24},{32,28},{36,32}... | collective-permute-start | bytes 3640328 | tf_op jit(solution)/shard_map/ppermute | solution.py:476
  8.0 36.3 %collective-permute-start.5 = (bf16[1040,128]{1,0:T(8,128)(2,1)}, bf16[1040,128]{1,0:T(8,128)(2,1)S(1)}, u32[]{:S(2)}, u32[]{:S(2)}) collective-permute-start(bf16[1040,128]{1,0:T(8,128)(2,1)} %weights.1.refs_9_.refs_13_), channel_id=1, source_target_pairs={{0,18},{1,19},{2,16},{3,17},{4,22},{5,23},{6,20},{7,21},{8,26},{9,... | collective-permute-start | bytes 798728 | tf_op jit(solution)/shard_map/ppermute | solution.py:469
  11.0 9.7 %collective-permute-start.11 = (bf16[128,512]{1,0:T(8,128)(2,1)S(1)}, bf16[128,512]{1,0:T(8,128)(2,1)S(1)}, u32[]{:S(2)}, u32[]{:S(2)}) collective-permute-start(bf16[128,512]{1,0:T(8,128)(2,1)S(1)} %copy-done.10), channel_id=1, source_target_pairs={{0,18},{1,19},{2,16},{3,17},{4,22},{5,23},{6,20},{7,21},{8,26},{9,... | collective-permute-start | bytes 393224 | tf_op jit(solution)/shard_map/ppermute | solution.py:483
  11.3 33.1 %collective-permute-start.8 = (bf16[640,128]{1,0:T(8,128)(2,1)S(1)}, bf16[640,128]{1,0:T(8,128)(2,1)S(1)}, u32[]{:S(2)}, u32[]{:S(2)}) collective-permute-start(bf16[640,128]{1,0:T(8,128)(2,1)S(1)} %copy-done.2), channel_id=1, source_target_pairs={{0,2},{1,3},{2,0},{3,1},{4,6},{5,7},{6,4},{7,5},{8,10},{9,11},{10,... | collective-permute-start | bytes 491528 | tf_op jit(solution)/shard_map/ppermute | solution.py:470
  20.7 48.6 %copy-start.11 = (bf16[128,512]{1,0:T(8,128)(2,1)}, bf16[128,512]{1,0:T(8,128)(2,1)S(1)}, u32[]{:S(2)}) copy-start(bf16[128,512]{1,0:T(8,128)(2,1)S(1)} %collective-permute-done.11.refs_23_) | copy-start | bytes 393220
  20.7 24.1 %collective-permute-start.7 = (bf16[640,128]{1,0:T(8,128)(2,1)S(1)}, bf16[640,128]{1,0:T(8,128)(2,1)S(1)}, u32[]{:S(2)}, u32[]{:S(2)}) collective-permute-start(bf16[640,128]{1,0:T(8,128)(2,1)S(1)} %copy-done.2), channel_id=1, source_target_pairs={{0,1},{1,0},{2,3},{3,2},{4,5},{5,4},{6,7},{7,6},{8,9},{9,8},{10,11... | collective-permute-start | bytes 491528 | tf_op jit(solution)/shard_map/ppermute | solution.py:481
  33.2 36.1 %copy-start = (bf16[474,1280]{1,0:T(8,128)(2,1)}, bf16[474,1280]{1,0:T(8,128)(2,1)S(1)}, u32[]{:S(2)}) copy-start(bf16[474,1280]{1,0:T(8,128)(2,1)S(1)} %collective-permute-done.refs_4_) | copy-start | bytes 3640324
  33.2 36.2 %collective-permute-start.1 = (bf16[474,1280]{1,0:T(8,128)(2,1)S(1)}, bf16[474,1280]{1,0:T(8,128)(2,1)}, u32[]{:S(2)}, u32[]{:S(2)}) collective-permute-start(bf16[474,1280]{1,0:T(8,128)(2,1)S(1)} %collective-permute-done.refs_4_), channel_id=1, source_target_pairs={{0,1},{1,0},{2,3},{3,2},{4,5},{5,4},{6,7},{7,6},{8,9},{9,8},{10,11... | collective-permute-start | bytes 3640328 | tf_op jit(solution)/shard_map/ppermute | solution.py:477
  36.6 32.7 %copy-start.1 = (bf16[474,1280]{1,0:T(8,128)(2,1)}, bf16[474,1280]{1,0:T(8,128)(2,1)S(1)}, u32[]{:S(2)}) copy-start(bf16[474,1280]{1,0:T(8,128)(2,1)S(1)} %collective-permute-done.2.refs_6_) | copy-start | bytes 3640324
  36.6 32.8 %collective-permute-start.3 = (bf16[474,1280]{1,0:T(8,128)(2,1)S(1)}, bf16[474,1280]{1,0:T(8,128)(2,1)}, u32[]{:S(2)}, u32[]{:S(2)}) collective-permute-start(bf16[474,1280]{1,0:T(8,128)(2,1)S(1)} %collective-permute-done.2.refs_6_), channel_id=1, source_target_pairs={{0,1},{1,0},{2,3},{3,2},{4,5},{5,4},{6,7},{7,6},{8,9},{9,8},{10,11... | collective-permute-start | bytes 3640328 | tf_op jit(solution)/shard_map/ppermute | solution.py:478
  44.3 2.5 %copy-start.7 = (bf16[640,128]{1,0:T(8,128)(2,1)}, bf16[640,128]{1,0:T(8,128)(2,1)S(1)}, u32[]{:S(2)}) copy-start(bf16[640,128]{1,0:T(8,128)(2,1)S(1)} %collective-permute-done.8.refs_15_.refs_19_) | copy-start | bytes 491524
  44.3 1.8 %collective-permute-start.4 = (bf16[1040,128]{1,0:T(8,128)(2,1)}, bf16[1040,128]{1,0:T(8,128)(2,1)S(1)}, u32[]{:S(2)}, u32[]{:S(2)}) collective-permute-start(bf16[1040,128]{1,0:T(8,128)(2,1)} %weights.1.refs_9_.refs_13_), channel_id=1, source_target_pairs={{0,1},{1,0},{2,3},{3,2},{4,5},{5,4},{6,7},{7,6},{8,9},{9,8},{10,11... | collective-permute-start | bytes 798728 | tf_op jit(solution)/shard_map/ppermute | solution.py:479
  44.3 2.5 %copy-start.4 = (bf16[1040,128]{1,0:T(8,128)(2,1)}, bf16[1040,128]{1,0:T(8,128)(2,1)S(1)}, u32[]{:S(2)}) copy-start(bf16[1040,128]{1,0:T(8,128)(2,1)S(1)} %collective-permute-done.5.refs_11_.refs_15_) | copy-start | bytes 798724
  44.3 2.5 %collective-permute-start.6 = (bf16[1040,128]{1,0:T(8,128)(2,1)S(1)}, bf16[1040,128]{1,0:T(8,128)(2,1)S(1)}, u32[]{:S(2)}, u32[]{:S(2)}) collective-permute-start(bf16[1040,128]{1,0:T(8,128)(2,1)S(1)} %collective-permute-done.5.refs_11_.refs_15_), channel_id=1, source_target_pairs={{0,1},{1,0},{2,3},{3,2},{4,5},{5,4},{6,7},{7,6},{8,9},{9,8},{10,11... | collective-permute-start | bytes 798728 | tf_op jit(solution)/shard_map/ppermute | solution.py:480
  44.8 2.0 %copy-start.8 = (bf16[640,128]{1,0:T(8,128)(2,1)}, bf16[640,128]{1,0:T(8,128)(2,1)S(1)}, u32[]{:S(2)}) copy-start(bf16[640,128]{1,0:T(8,128)(2,1)S(1)} %collective-permute-done.7.refs_14_.refs_18_) | copy-start | bytes 491524
  44.8 1.8 %collective-permute-start.9 = (bf16[640,128]{1,0:T(8,128)(2,1)S(1)}, bf16[640,128]{1,0:T(8,128)(2,1)S(1)}, u32[]{:S(2)}, u32[]{:S(2)}) collective-permute-start(bf16[640,128]{1,0:T(8,128)(2,1)S(1)} %collective-permute-done.8.refs_15_.refs_19_), channel_id=1, source_target_pairs={{0,1},{1,0},{2,3},{3,2},{4,5},{5,4},{6,7},{7,6},{8,9},{9,8},{10,11... | collective-permute-start | bytes 491528 | tf_op jit(solution)/shard_map/ppermute | solution.py:482
  46.1 0.8 copy-start.5
  46.1 23.3 %collective-permute-start.10 = (bf16[128,512]{1,0:T(8,128)(2,1)S(1)}, bf16[128,512]{1,0:T(8,128)(2,1)}, u32[]{:S(2)}, u32[]{:S(2)}) collective-permute-start(bf16[128,512]{1,0:T(8,128)(2,1)S(1)} %copy-done.10), channel_id=1, source_target_pairs={{0,1},{1,0},{2,3},{3,2},{4,5},{5,4},{6,7},{7,6},{8,9},{9,8},{10,11... | collective-permute-start | bytes 393224 | tf_op jit(solution)/shard_map/ppermute | solution.py:484
  46.7 0.7 copy-start.9
  46.7 22.7 %collective-permute-start.12 = (bf16[128,512]{1,0:T(8,128)(2,1)S(1)}, bf16[128,512]{1,0:T(8,128)(2,1)}, u32[]{:S(2)}, u32[]{:S(2)}) collective-permute-start(bf16[128,512]{1,0:T(8,128)(2,1)S(1)} %collective-permute-done.11.refs_23_), channel_id=1, source_target_pairs={{0,1},{1,0},{2,3},{3,2},{4,5},{5,4},{6,7},{7,6},{8,9},{9,8},{10,11... | collective-permute-start | bytes 393224 | tf_op jit(solution)/shard_map/ppermute | solution.py:485
  46.8 0.7 copy-start.6
  86.3 19.4 %copy-start.3 = (bf16[640,128]{1,0:T(8,128)(2,1)S(1)}, bf16[640,128]{1,0:T(8,128)(2,1)}, u32[]{:S(2)}) copy-start(bf16[640,128]{1,0:T(8,128)(2,1)} %refs_17_.1) | copy-start | bytes 491524
  86.3 19.4 %copy-start.12 = (f32[128]{0:T(128)S(1)}, f32[128]{0:T(128)}, u32[]{:S(2)}) copy-start(f32[128]{0:T(128)} %param.29) | copy-start | bytes 1540
  86.3 19.4 %copy-start.13 = (f32[128]{0:T(128)S(1)}, f32[128]{0:T(128)}, u32[]{:S(2)}) copy-start(f32[128]{0:T(128)} %param.28) | copy-start | bytes 1540
  86.3 1.9 %collective-permute-start.14 = (f32[640,128]{1,0:T(8,128)}, f32[640,128]{1,0:T(8,128)S(1)}, u32[]{:S(2)}, u32[]{:S(2)}) collective-permute-start(f32[640,128]{1,0:T(8,128)} %get-tuple-element.28), channel_id=1, source_target_pairs={{0,1},{1,0},{2,3},{3,2},{4,5},{5,4},{6,7},{7,6},{8,9},{9,8},{10,11... | collective-permute-start | bytes 983048 | tf_op jit(solution)/shard_map/ppermute | solution.py:508
  86.5 3.7 %collective-permute-start.13 = (f32[640,128]{1,0:T(8,128)}, f32[640,128]{1,0:T(8,128)S(1)}, u32[]{:S(2)}, u32[]{:S(2)}) collective-permute-start(f32[640,128]{1,0:T(8,128)} %get-tuple-element.26), channel_id=1, source_target_pairs={{0,1},{1,0},{2,3},{3,2},{4,5},{5,4},{6,7},{7,6},{8,9},{9,8},{10,11... | collective-permute-start | bytes 983048 | tf_op jit(solution)/shard_map/ppermute | solution.py:510
  89.3 7.8 %collective-permute-start.15 = (bf16[640,128]{1,0:T(8,128)(2,1)S(1)}, bf16[640,128]{1,0:T(8,128)(2,1)S(1)}, u32[]{:S(2)}, u32[]{:S(2)}) collective-permute-start(bf16[640,128]{1,0:T(8,128)(2,1)S(1)} %add_convert_fusion.1), channel_id=1, source_target_pairs={{0,2},{1,3},{2,0},{3,1},{4,6},{5,7},{6,4},{7,5},{8,10},{9,11},{10,... | collective-permute-start | bytes 491528 | tf_op jit(solution)/shard_map/ppermute | solution.py:509
where the time goes:
time: 107 us
  Pallas kernels  44.5 us (42%)
  waiting for transfers between devices  41 us (38%)
  starting transfers between devices  9.66 us (9%)
  blocking collectives  7.25 us (7%)
  other arithmetic  3.2 us (3%)
    pallas_call x2, Pallas kernels, block_call(): pl.pallas_call(functools.partial(block_kernel, outer, chunks, own_columns...  38.6 us
    ppermute x1, waiting for transfers between devices, encoder(): low_own = lax.ppermute(low_half, 'lon', forward)  12.4 us
    ppermute x1, waiting for transfers between devices, encoder(): mesh_far = lax.ppermute(mesh_latent, 'ch', across)  7.72 us
    ppermute x1, waiting for transfers between devices, encoder(): message_far = lax.ppermute(message_weight, ('lon', 'ch'), facing)  7.49 us
    psum x1, blocking collectives, encoder(): lax.psum((jnp.sum(node_share, axis=1, keepdims=True), jnp.sum(jnp.square(...  7.25 us
    ppermute x1, waiting for transfers between devices, encoder(): far = lax.ppermute(far.astype(bf16), 'ch', across).astype(f32)  6.95 us
    pallas_call x1, Pallas kernels, pack_call(): pl.pallas_call(functools.partial(pack_kernel, chunks, points_own, all_poi...  4.12 us
    ppermute x1, waiting for transfers between devices, encoder(): high_own = lax.ppermute(high_half, 'lon', backward)  3.41 us
  transfers between devices with their start and end apart: 16, of which 8 were waited for; matrix products, arithmetic and copies ran while one was open for 1% of the time, Pallas kernels for 22%

commit v1 on v0

--- a/solution.py
+++ b/solution.py
@@ -312,20 +312,32 @@
 
 
 def pack_kernel(chunks, points_own, all_points, nodes, lon_ref, place, senders, receivers, grid,
-                points, ids, low_ref, high_ref, low_half, high_half, sems):
+                points, ids, low_ref, high_ref, low_half, high_half, pieces, sems):
     lon = lon_ref[0]
     k = place[0]
     half = HALO * LAT // 2
     side = lax.bitwise_and(k, 1) * half
     low_at = pl.multiple_of(points_own - 2 * half + side, 128)
-    copies = [
-        pltpu.make_async_copy(grid.at[:, pl.ds(low_at, half)], low_half, sems.at[0]),
-        pltpu.make_async_copy(
-            grid.at[:, pl.ds(pl.multiple_of(side, 128), half)], high_half, sems.at[1]
-        ),
-    ]
-    for copy in copies:
-        copy.start()
+    copies = []
+    for n, (source_at, target, target_at) in enumerate(
+        (begin + step, target, step)
+        for begin, target in ((low_at, low_half), (side, high_half))
+        for step in (0, LAT)
+    ):
+        copies.append(
+            (
+                pltpu.make_async_copy(
+                    grid.at[:, pl.ds(pl.multiple_of(source_at, 128), LAT)],
+                    pieces.at[n],
+                    sems.at[n],
+                ),
+                pltpu.make_async_copy(
+                    pieces.at[n], target.at[:, pl.ds(target_at, LAT)], sems.at[4 + n]
+                ),
+            )
+        )
+    for first, _ in copies:
+        first.start()
     for i in range(chunks):
         rows = pl.ds(pl.multiple_of((k * chunks + i) * 4, 4), 4)
         point = senders[rows, :] - lon * points_own + HALO * LAT
@@ -335,8 +347,11 @@
         ids[i * 4 : i * 4 + 4, :] = (receivers[rows, :] - lon * nodes) * 4
         for ref, end in ((low_ref, jnp.min(point)), (high_ref, jnp.max(point))):
             ref[i] = lax.shift_right_logical(lax.shift_right_logical(end, 7) * 13108, 16)
-    for copy in copies:
-        copy.wait()
+    for first, then in copies:
+        first.wait()
+        then.start()
+    for _, then in copies:
+        then.wait()
 
 
 def weights_call(share, operands):
@@ -358,8 +373,11 @@
         functools.partial(pack_kernel, chunks, points_own, all_points, nodes),
         out_shape=(index, index, ends, ends, side, side),
         in_specs=[SMEM] * 2 + [VMEM] * 2 + [ANY],
-        out_specs=(VMEM, VMEM, SMEM, SMEM, VMEM, VMEM),
-        scratch_shapes=[pltpu.SemaphoreType.DMA((2,))],
+        out_specs=(VMEM, VMEM, SMEM, SMEM, ANY, ANY),
+        scratch_shapes=[
+            pltpu.VMEM((4, channels, LAT), bf16),
+            pltpu.SemaphoreType.DMA((8,)),
+        ],
         name="pack",
     )(*operands)
 
@@ -508,13 +526,8 @@
     far = keep_far + lax.ppermute(send_far, "ch", swap)
     far = lax.ppermute(far.astype(bf16), "ch", across).astype(f32)
     node_share = keep_here + lax.ppermute(send_here, "ch", swap) + far
-    first_sum, second = lax.psum(
-        (
-            jnp.sum(node_share, axis=1, keepdims=True),
-            jnp.sum(jnp.square(node_share), axis=1, keepdims=True),
-        ),
-        "ch",
-    )
+    sums = jnp.stack([jnp.sum(node_share, axis=1), jnp.sum(jnp.square(node_share), axis=1)])
+    first_sum, second = jnp.sum(lax.all_gather(sums, "ch"), axis=0)[:, :, None]
     centre = first_sum / full_width
     spread = second / full_width - jnp.square(centre)
     normed = (node_share - centre) * lax.rsqrt(spread + 1.0)

time: 107 us -> 107 us (level)
    psum x1 -> x0, blocking collectives: 7.25 us -> none  [encoder(): lax.psum((jnp.sum(node_share, axis=1, keepdims=True), jnp.sum(jnp.square(...]
    all_gather x0 -> x1, blocking collectives: none -> 6.72 us  [encoder(): first_sum, second = jnp.sum(lax.all_gather(sums, 'ch'), axis=0)[:, :, None]]
where the time goes in v1:
time: 107 us; the launch traced here: 106 us
  Pallas kernels  44.6 us (42%)
  waiting for transfers between devices  41 us (38%)
  starting transfers between devices  9.63 us (9%)
  blocking collectives  6.72 us (6%)
  other arithmetic  3.24 us (3%)
    pallas_call x2, Pallas kernels, block_call(): pl.pallas_call(functools.partial(block_kernel, outer, chunks, own_columns...  38.6 us
    ppermute x1, waiting for transfers between devices, encoder(): low_own = lax.ppermute(low_half, 'lon', forward)  12.4 us
    ppermute x1, waiting for transfers between devices, encoder(): mesh_far = lax.ppermute(mesh_latent, 'ch', across)  7.73 us
    ppermute x1, waiting for transfers between devices, encoder(): message_far = lax.ppermute(message_weight, ('lon', 'ch'), facing)  7.48 us
    ppermute x1, waiting for transfers between devices, encoder(): far = lax.ppermute(far.astype(bf16), 'ch', across).astype(f32)  6.98 us
    all_gather x1, blocking collectives, encoder(): first_sum, second = jnp.sum(lax.all_gather(sums, 'ch'), axis=0)[:, :, None]  6.72 us
    pallas_call x1, Pallas kernels, pack_call(): pl.pallas_call(functools.partial(pack_kernel, chunks, points_own, all_poi...  4.2 us
    ppermute x1, waiting for transfers between devices, encoder(): high_own = lax.ppermute(high_half, 'lon', backward)  3.41 us
  transfers between devices with their start and end apart: 16, of which 8 were waited for; matrix products, arithmetic and copies ran while one was open for 1% of the time, Pallas kernels for 22%

profile of v1, /device:TPU:6, one launch (start us, length us, event | category | flops | bytes accessed | tf_op | source)
XLA Modules:
  0.0 106.2 jit_solution(7861897548794879312)
XLA Ops:
  0.0 0.0 copy-start.10
  0.0 0.0 copy-start.2
  0.0 4.2 %pack.1 = (s32[44,128]{1,0:T(8,128)}, s32[44,128]{1,0:T(8,128)}, s32[11]{0:T(128)}, s32[11]{0:T(128)}, bf16[474,1280]{1,0:T(8,128)(2,1)}, /*index=5*/bf16[474,1280]{1,0:T(8,128)(2,1)}) custom-call(s32[1]{0:T(128)} %bitcast.1.lon_ref, s32[1]{0:T(128)} %bitcast.place.refs_0_, s32[176,128]{1,0:T(8,128)} %bitcast.18, s32[176,128]{1,0:T(8,128)} %bitcast.19, ...), custom_call_target="tpu_custom_call" | custom-call | tf_op jit(solution)/shard_map/pack/pallas_call | solution.py:372
  4.2 1.6 %collective-permute-start = (bf16[474,1280]{1,0:T(8,128)(2,1)}, bf16[474,1280]{1,0:T(8,128)(2,1)S(1)}, u32[]{:S(2)}, u32[]{:S(2)}) collective-permute-start(bf16[474,1280]{1,0:T(8,128)(2,1)} %get-tuple-element.19), channel_id=1, source_target_pairs={{0,4},{4,8},{8,12},{12,16},{16,20},{20,24},{24,28},{28,32},{32,36}... | collective-permute-start | bytes 3640328 | tf_op jit(solution)/shard_map/ppermute | solution.py:493
  5.8 0.5 collective-permute-start.2
  6.3 1.8 %weights.1.refs_9_.refs_13_ = bf16[1040,128]{1,0:T(8,128)(2,1)} custom-call(bf16[4,128]{1,0:T(4,128)(2,1)} %feature_weight.1, f32[1,128]{1,0:T(1,128)} %bitcast.23, bf16[512,128]{1,0:T(8,128)(2,1)} %sender_weight.1, bf16[512,128]{1,0:T(8,128)(2,1)} %receiver_weight.1), custom_call_target="tpu_custom_call" | custom-call | tf_op jit(solution)/shard_map/weights/pallas_call | solution.py:358
  8.1 3.0 %collective-permute-start.5 = (bf16[1040,128]{1,0:T(8,128)(2,1)}, bf16[1040,128]{1,0:T(8,128)(2,1)S(1)}, u32[]{:S(2)}, u32[]{:S(2)}) collective-permute-start(bf16[1040,128]{1,0:T(8,128)(2,1)} %weights.1.refs_9_.refs_13_), channel_id=1, source_target_pairs={{0,18},{1,19},{2,16},{3,17},{4,22},{5,23},{6,20},{7,21},{8,26},{9,... | collective-permute-start | bytes 798728 | tf_op jit(solution)/shard_map/ppermute | solution.py:487
  11.1 0.0 copy-done.10
  11.1 0.2 collective-permute-start.11
  11.3 0.0 copy-done.2
  11.3 2.0 %collective-permute-start.8 = (bf16[640,128]{1,0:T(8,128)(2,1)S(1)}, bf16[640,128]{1,0:T(8,128)(2,1)S(1)}, u32[]{:S(2)}, u32[]{:S(2)}) collective-permute-start(bf16[640,128]{1,0:T(8,128)(2,1)S(1)} %copy-done.2), channel_id=1, source_target_pairs={{0,2},{1,3},{2,0},{3,1},{4,6},{5,7},{6,4},{7,5},{8,10},{9,11},{10,... | collective-permute-start | bytes 491528 | tf_op jit(solution)/shard_map/ppermute | solution.py:488
  13.3 7.5 %collective-permute-done.11.refs_23_ = bf16[128,512]{1,0:T(8,128)(2,1)S(1)} collective-permute-done((bf16[128,512]{1,0:T(8,128)(2,1)S(1)}, bf16[128,512]{1,0:T(8,128)(2,1)S(1)}, u32[]{:S(2)}, u32[]{:S(2)}) %collective-permute-start.11) | collective-permute-done | bytes 131104 | tf_op jit(solution)/shard_map/ppermute | solution.py:501
  20.8 0.0 copy-start.11
  20.8 0.0 collective-permute-start.7
  20.8 12.4 %collective-permute-done.refs_4_ = bf16[474,1280]{1,0:T(8,128)(2,1)S(1)} collective-permute-done((bf16[474,1280]{1,0:T(8,128)(2,1)}, bf16[474,1280]{1,0:T(8,128)(2,1)S(1)}, u32[]{:S(2)}, u32[]{:S(2)}) %collective-permute-start) | collective-permute-done | bytes 1213472 | tf_op jit(solution)/shard_map/ppermute | solution.py:493
  33.3 0.0 collective-permute-start.1
  33.3 3.4 %collective-permute-done.2.refs_6_ = bf16[474,1280]{1,0:T(8,128)(2,1)S(1)} collective-permute-done((bf16[474,1280]{1,0:T(8,128)(2,1)}, bf16[474,1280]{1,0:T(8,128)(2,1)S(1)}, u32[]{:S(2)}, u32[]{:S(2)}) %collective-permute-start.2) | collective-permute-done | bytes 1213472 | tf_op jit(solution)/shard_map/ppermute | solution.py:494
  36.7 0.0 collective-permute-start.3
  36.7 7.7 %collective-permute-done.8.refs_15_.refs_19_ = bf16[640,128]{1,0:T(8,128)(2,1)S(1)} collective-permute-done((bf16[640,128]{1,0:T(8,128)(2,1)S(1)}, bf16[640,128]{1,0:T(8,128)(2,1)S(1)}, u32[]{:S(2)}, u32[]{:S(2)}) %collective-permute-start.8) | collective-permute-done | bytes 163872 | tf_op jit(solution)/shard_map/ppermute | solution.py:488
  44.4 0.0 copy-start.7
  44.4 0.0 collective-permute-start.4
  44.4 0.0 collective-permute-done.5.refs_11_.refs_15_
  44.4 0.0 copy-start.4
  44.4 0.5 collective-permute-start.6
  44.9 0.0 collective-permute-done.7.refs_14_.refs_18_
  44.9 0.0 copy-start.8
  44.9 0.1 collective-permute-start.9
  45.0 1.1 %collective-permute-done.4.refs_10_.refs_14_ = bf16[1040,128]{1,0:T(8,128)(2,1)S(1)} collective-permute-done((bf16[1040,128]{1,0:T(8,128)(2,1)}, bf16[1040,128]{1,0:T(8,128)(2,1)S(1)}, u32[]{:S(2)}, u32[]{:S(2)}) %collective-permute-start.4) | collective-permute-done | bytes 266272 | tf_op jit(solution)/shard_map/ppermute | solution.py:497
  46.2 0.0 copy-start.5
  46.2 0.1 collective-permute-start.10
  46.3 0.5 collective-permute-done.9.refs_16_.refs_20_
  46.8 0.1 collective-permute-start.12
  46.9 0.0 collective-permute-done.6.refs_12_.refs_16_
  46.9 0.0 copy-done.7
  46.9 0.0 copy-done.4
  46.9 0.0 copy-done.8
  46.9 0.0 copy-done.5
  47.0 0.5 copy-done.9
  47.5 0.2 copy-done.6
  47.6 21.7 %block_inner.1 = (f32[640,512]{1,0:T(8,128)}, f32[640,128]{1,0:T(8,128)}) custom-call(s32[1]{0:T(128)} %bitcast.place.refs_0_, s32[11]{0:T(128)} %get-tuple-element.17.refs_1_, s32[11]{0:T(128)} %get-tuple-element.18.refs_2_, bf16[474,28800]{1,0:T(8,128)(2,1)} %bitcast.14, s32[44,128]{1,0:T(8,128)} %get-tuple-element.21.refs_4_.refs_8_, ...), custom_call_target="tpu_custom_call" | custom-call | flops 9596567552 | bytes 5767168 | tf_op jit(solution)/shard_map/block_inner/pallas_call | solution.py:403
  69.4 0.0 copy-done.11
  69.4 0.0 copy-done
  69.4 0.0 copy-done.1
  69.4 0.0 collective-permute-done.10.refs_22_
  69.4 0.0 collective-permute-done.12.refs_24_
  69.5 0.0 collective-permute-done.1.refs_5_
  69.5 0.0 collective-permute-done.3.refs_7_
  69.5 16.9 %block_outer.1 = (f32[640,128]{1,0:T(8,128)}, f32[640,128]{1,0:T(8,128)}, f32[640,128]{1,0:T(8,128)}, f32[640,128]{1,0:T(8,128)}) custom-call(s32[1]{0:T(128)} %bitcast.place.refs_0_, s32[11]{0:T(128)} %get-tuple-element.17.refs_1_, s32[11]{0:T(128)} %get-tuple-element.18.refs_2_, bf16[474,28800]{1,0:T(8,128)(2,1)} %bitcast.15, bf16[474,1280]{1,0:T(8,128)(2,1)} %copy-done, ...), custom_call_target="tpu_custom_call" | custom-call | flops 9596567552 | bytes 5767168 | tf_op jit(solution)/shard_map/block_outer/pallas_call | solution.py:403
  86.4 0.0 copy-start.3
  86.4 0.0 copy-start.12
  86.4 0.0 copy-start.13
  86.4 0.2 collective-permute-start.14
  86.6 0.4 collective-permute-start.13
  87.0 1.3 %collective-permute-done.14 = f32[640,128]{1,0:T(8,128)S(1)} collective-permute-done((f32[640,128]{1,0:T(8,128)}, f32[640,128]{1,0:T(8,128)S(1)}, u32[]{:S(2)}, u32[]{:S(2)}) %collective-permute-start.14) | collective-permute-done | bytes 327712 | tf_op jit(solution)/shard_map/ppermute | solution.py:526
  88.3 1.0 add_convert_fusion.1
  89.4 0.8 collective-permute-start.15
  90.2 0.0 collective-permute-done.13
  90.2 7.0 %collective-permute-done.15 = bf16[640,128]{1,0:T(8,128)(2,1)S(1)} collective-permute-done((bf16[640,128]{1,0:T(8,128)(2,1)S(1)}, bf16[640,128]{1,0:T(8,128)(2,1)S(1)}, u32[]{:S(2)}, u32[]{:S(2)}) %collective-permute-start.15) | collective-permute-done | bytes 163872 | tf_op jit(solution)/shard_map/ppermute | solution.py:527
  97.2 1.2 %fusion.2 = (f32[640]{0:T(1024)S(1)}, f32[640]{0:T(1024)S(1)}, f32[640,128]{1,0:T(8,128)S(1)}) fusion(bf16[640,128]{1,0:T(8,128)(2,1)S(1)} %collective-permute-done.15, f32[640,128]{1,0:T(8,128)} %get-tuple-element.25, f32[640,128]{1,0:T(8,128)S(1)} %collective-permute-done.13), kind=kLoop, calls=%fused_computation.10 | loop fusion | flops 490240 | bytes 1152000 | tf_op jit(solution)/shard_map/reduce_sum | solution.py:529
  98.5 6.7 %all-gather.1 = f32[4,2,640]{2,1,0:T(2,128)S(1)} all-gather(f32[1,2,640]{2,1,0:T(2,128)S(1)} %maximum_bitcast_fusion), channel_id=2, replica_groups=mesh['lon'=32,'ch'=4] {'ch'}, dimensions={0}, use_global_device_ids=true | all-gather | bytes 25600 | tf_op jit(solution)/shard_map/all_gather | solution.py:530
  105.2 0.0 copy-done.3
  105.3 0.0 copy-done.12
  105.3 0.0 copy-done.13
  105.3 0.9 add_convert_fusion
  (10 shorter events, 0.1 us)
Async XLA Ops:
  0.0 11.1 %copy-start.10 = (bf16[128,512]{1,0:T(8,128)(2,1)S(1)}, bf16[128,512]{1,0:T(8,128)(2,1)}, u32[]{:S(2)}) copy-start(bf16[128,512]{1,0:T(8,128)(2,1)} %refs_21_.1) | copy-start | bytes 393220
  0.0 11.3 %copy-start.2 = (bf16[640,128]{1,0:T(8,128)(2,1)S(1)}, bf16[640,128]{1,0:T(8,128)(2,1)}, u32[]{:S(2)}) copy-start(bf16[640,128]{1,0:T(8,128)(2,1)} %refs_17_.1) | copy-start | bytes 491524
  4.2 29.0 %collective-permute-start = (bf16[474,1280]{1,0:T(8,128)(2,1)}, bf16[474,1280]{1,0:T(8,128)(2,1)S(1)}, u32[]{:S(2)}, u32[]{:S(2)}) collective-permute-start(bf16[474,1280]{1,0:T(8,128)(2,1)} %get-tuple-element.19), channel_id=1, source_target_pairs={{0,4},{4,8},{8,12},{12,16},{16,20},{20,24},{24,28},{28,32},{32,36}... | collective-permute-start | bytes 3640328 | tf_op jit(solution)/shard_map/ppermute | solution.py:493
  5.8 30.9 %collective-permute-start.2 = (bf16[474,1280]{1,0:T(8,128)(2,1)}, bf16[474,1280]{1,0:T(8,128)(2,1)S(1)}, u32[]{:S(2)}, u32[]{:S(2)}) collective-permute-start(bf16[474,1280]{1,0:T(8,128)(2,1)} %get-tuple-element.20), channel_id=1, source_target_pairs={{4,0},{8,4},{12,8},{16,12},{20,16},{24,20},{28,24},{32,28},{36,32}... | collective-permute-start | bytes 3640328 | tf_op jit(solution)/shard_map/ppermute | solution.py:494
  8.1 36.3 %collective-permute-start.5 = (bf16[1040,128]{1,0:T(8,128)(2,1)}, bf16[1040,128]{1,0:T(8,128)(2,1)S(1)}, u32[]{:S(2)}, u32[]{:S(2)}) collective-permute-start(bf16[1040,128]{1,0:T(8,128)(2,1)} %weights.1.refs_9_.refs_13_), channel_id=1, source_target_pairs={{0,18},{1,19},{2,16},{3,17},{4,22},{5,23},{6,20},{7,21},{8,26},{9,... | collective-permute-start | bytes 798728 | tf_op jit(solution)/shard_map/ppermute | solution.py:487
  11.1 9.7 %collective-permute-start.11 = (bf16[128,512]{1,0:T(8,128)(2,1)S(1)}, bf16[128,512]{1,0:T(8,128)(2,1)S(1)}, u32[]{:S(2)}, u32[]{:S(2)}) collective-permute-start(bf16[128,512]{1,0:T(8,128)(2,1)S(1)} %copy-done.10), channel_id=1, source_target_pairs={{0,18},{1,19},{2,16},{3,17},{4,22},{5,23},{6,20},{7,21},{8,26},{9,... | collective-permute-start | bytes 393224 | tf_op jit(solution)/shard_map/ppermute | solution.py:501
  11.3 33.1 %collective-permute-start.8 = (bf16[640,128]{1,0:T(8,128)(2,1)S(1)}, bf16[640,128]{1,0:T(8,128)(2,1)S(1)}, u32[]{:S(2)}, u32[]{:S(2)}) collective-permute-start(bf16[640,128]{1,0:T(8,128)(2,1)S(1)} %copy-done.2), channel_id=1, source_target_pairs={{0,2},{1,3},{2,0},{3,1},{4,6},{5,7},{6,4},{7,5},{8,10},{9,11},{10,... | collective-permute-start | bytes 491528 | tf_op jit(solution)/shard_map/ppermute | solution.py:488
  20.8 48.6 %copy-start.11 = (bf16[128,512]{1,0:T(8,128)(2,1)}, bf16[128,512]{1,0:T(8,128)(2,1)S(1)}, u32[]{:S(2)}) copy-start(bf16[128,512]{1,0:T(8,128)(2,1)S(1)} %collective-permute-done.11.refs_23_) | copy-start | bytes 393220
  20.8 24.1 %collective-permute-start.7 = (bf16[640,128]{1,0:T(8,128)(2,1)S(1)}, bf16[640,128]{1,0:T(8,128)(2,1)S(1)}, u32[]{:S(2)}, u32[]{:S(2)}) collective-permute-start(bf16[640,128]{1,0:T(8,128)(2,1)S(1)} %copy-done.2), channel_id=1, source_target_pairs={{0,1},{1,0},{2,3},{3,2},{4,5},{5,4},{6,7},{7,6},{8,9},{9,8},{10,11... | collective-permute-start | bytes 491528 | tf_op jit(solution)/shard_map/ppermute | solution.py:499
  33.3 36.2 %copy-start = (bf16[474,1280]{1,0:T(8,128)(2,1)}, bf16[474,1280]{1,0:T(8,128)(2,1)S(1)}, u32[]{:S(2)}) copy-start(bf16[474,1280]{1,0:T(8,128)(2,1)S(1)} %collective-permute-done.refs_4_) | copy-start | bytes 3640324
  33.3 36.2 %collective-permute-start.1 = (bf16[474,1280]{1,0:T(8,128)(2,1)S(1)}, bf16[474,1280]{1,0:T(8,128)(2,1)}, u32[]{:S(2)}, u32[]{:S(2)}) collective-permute-start(bf16[474,1280]{1,0:T(8,128)(2,1)S(1)} %collective-permute-done.refs_4_), channel_id=1, source_target_pairs={{0,1},{1,0},{2,3},{3,2},{4,5},{5,4},{6,7},{7,6},{8,9},{9,8},{10,11... | collective-permute-start | bytes 3640328 | tf_op jit(solution)/shard_map/ppermute | solution.py:495
  36.7 32.7 %copy-start.1 = (bf16[474,1280]{1,0:T(8,128)(2,1)}, bf16[474,1280]{1,0:T(8,128)(2,1)S(1)}, u32[]{:S(2)}) copy-start(bf16[474,1280]{1,0:T(8,128)(2,1)S(1)} %collective-permute-done.2.refs_6_) | copy-start | bytes 3640324
  36.7 32.8 %collective-permute-start.3 = (bf16[474,1280]{1,0:T(8,128)(2,1)S(1)}, bf16[474,1280]{1,0:T(8,128)(2,1)}, u32[]{:S(2)}, u32[]{:S(2)}) collective-permute-start(bf16[474,1280]{1,0:T(8,128)(2,1)S(1)} %collective-permute-done.2.refs_6_), channel_id=1, source_target_pairs={{0,1},{1,0},{2,3},{3,2},{4,5},{5,4},{6,7},{7,6},{8,9},{9,8},{10,11... | collective-permute-start | bytes 3640328 | tf_op jit(solution)/shard_map/ppermute | solution.py:496
  44.4 2.5 %copy-start.7 = (bf16[640,128]{1,0:T(8,128)(2,1)}, bf16[640,128]{1,0:T(8,128)(2,1)S(1)}, u32[]{:S(2)}) copy-start(bf16[640,128]{1,0:T(8,128)(2,1)S(1)} %collective-permute-done.8.refs_15_.refs_19_) | copy-start | bytes 491524
  44.4 1.8 %collective-permute-start.4 = (bf16[1040,128]{1,0:T(8,128)(2,1)}, bf16[1040,128]{1,0:T(8,128)(2,1)S(1)}, u32[]{:S(2)}, u32[]{:S(2)}) collective-permute-start(bf16[1040,128]{1,0:T(8,128)(2,1)} %weights.1.refs_9_.refs_13_), channel_id=1, source_target_pairs={{0,1},{1,0},{2,3},{3,2},{4,5},{5,4},{6,7},{7,6},{8,9},{9,8},{10,11... | collective-permute-start | bytes 798728 | tf_op jit(solution)/shard_map/ppermute | solution.py:497
  44.4 2.5 %copy-start.4 = (bf16[1040,128]{1,0:T(8,128)(2,1)}, bf16[1040,128]{1,0:T(8,128)(2,1)S(1)}, u32[]{:S(2)}) copy-start(bf16[1040,128]{1,0:T(8,128)(2,1)S(1)} %collective-permute-done.5.refs_11_.refs_15_) | copy-start | bytes 798724
  44.4 2.5 %collective-permute-start.6 = (bf16[1040,128]{1,0:T(8,128)(2,1)S(1)}, bf16[1040,128]{1,0:T(8,128)(2,1)S(1)}, u32[]{:S(2)}, u32[]{:S(2)}) collective-permute-start(bf16[1040,128]{1,0:T(8,128)(2,1)S(1)} %collective-permute-done.5.refs_11_.refs_15_), channel_id=1, source_target_pairs={{0,1},{1,0},{2,3},{3,2},{4,5},{5,4},{6,7},{7,6},{8,9},{9,8},{10,11... | collective-permute-start | bytes 798728 | tf_op jit(solution)/shard_map/ppermute | solution.py:498
  44.9 2.0 %copy-start.8 = (bf16[640,128]{1,0:T(8,128)(2,1)}, bf16[640,128]{1,0:T(8,128)(2,1)S(1)}, u32[]{:S(2)}) copy-start(bf16[640,128]{1,0:T(8,128)(2,1)S(1)} %collective-permute-done.7.refs_14_.refs_18_) | copy-start | bytes 491524
  44.9 1.8 %collective-permute-start.9 = (bf16[640,128]{1,0:T(8,128)(2,1)S(1)}, bf16[640,128]{1,0:T(8,128)(2,1)S(1)}, u32[]{:S(2)}, u32[]{:S(2)}) collective-permute-start(bf16[640,128]{1,0:T(8,128)(2,1)S(1)} %collective-permute-done.8.refs_15_.refs_19_), channel_id=1, source_target_pairs={{0,1},{1,0},{2,3},{3,2},{4,5},{5,4},{6,7},{7,6},{8,9},{9,8},{10,11... | collective-permute-start | bytes 491528 | tf_op jit(solution)/shard_map/ppermute | solution.py:500
  46.2 0.8 copy-start.5
  46.2 23.3 %collective-permute-start.10 = (bf16[128,512]{1,0:T(8,128)(2,1)S(1)}, bf16[128,512]{1,0:T(8,128)(2,1)}, u32[]{:S(2)}, u32[]{:S(2)}) collective-permute-start(bf16[128,512]{1,0:T(8,128)(2,1)S(1)} %copy-done.10), channel_id=1, source_target_pairs={{0,1},{1,0},{2,3},{3,2},{4,5},{5,4},{6,7},{7,6},{8,9},{9,8},{10,11... | collective-permute-start | bytes 393224 | tf_op jit(solution)/shard_map/ppermute | solution.py:502
  46.8 0.7 copy-start.9
  46.8 22.7 %collective-permute-start.12 = (bf16[128,512]{1,0:T(8,128)(2,1)S(1)}, bf16[128,512]{1,0:T(8,128)(2,1)}, u32[]{:S(2)}, u32[]{:S(2)}) collective-permute-start(bf16[128,512]{1,0:T(8,128)(2,1)S(1)} %collective-permute-done.11.refs_23_), channel_id=1, source_target_pairs={{0,1},{1,0},{2,3},{3,2},{4,5},{5,4},{6,7},{7,6},{8,9},{9,8},{10,11... | collective-permute-start | bytes 393224 | tf_op jit(solution)/shard_map/ppermute | solution.py:503
  46.9 0.7 copy-start.6
  86.4 18.9 %copy-start.3 = (bf16[640,128]{1,0:T(8,128)(2,1)S(1)}, bf16[640,128]{1,0:T(8,128)(2,1)}, u32[]{:S(2)}) copy-start(bf16[640,128]{1,0:T(8,128)(2,1)} %refs_17_.1) | copy-start | bytes 491524
  86.4 18.9 %copy-start.12 = (f32[128]{0:T(128)S(1)}, f32[128]{0:T(128)}, u32[]{:S(2)}) copy-start(f32[128]{0:T(128)} %param.29) | copy-start | bytes 1540
  86.4 18.9 %copy-start.13 = (f32[128]{0:T(128)S(1)}, f32[128]{0:T(128)}, u32[]{:S(2)}) copy-start(f32[128]{0:T(128)} %param.28) | copy-start | bytes 1540
  86.4 1.9 %collective-permute-start.14 = (f32[640,128]{1,0:T(8,128)}, f32[640,128]{1,0:T(8,128)S(1)}, u32[]{:S(2)}, u32[]{:S(2)}) collective-permute-start(f32[640,128]{1,0:T(8,128)} %get-tuple-element.28), channel_id=1, source_target_pairs={{0,1},{1,0},{2,3},{3,2},{4,5},{5,4},{6,7},{7,6},{8,9},{9,8},{10,11... | collective-permute-start | bytes 983048 | tf_op jit(solution)/shard_map/ppermute | solution.py:526
  86.6 3.6 %collective-permute-start.13 = (f32[640,128]{1,0:T(8,128)}, f32[640,128]{1,0:T(8,128)S(1)}, u32[]{:S(2)}, u32[]{:S(2)}) collective-permute-start(f32[640,128]{1,0:T(8,128)} %get-tuple-element.26), channel_id=1, source_target_pairs={{0,1},{1,0},{2,3},{3,2},{4,5},{5,4},{6,7},{7,6},{8,9},{9,8},{10,11... | collective-permute-start | bytes 983048 | tf_op jit(solution)/shard_map/ppermute | solution.py:528
  89.4 7.8 %collective-permute-start.15 = (bf16[640,128]{1,0:T(8,128)(2,1)S(1)}, bf16[640,128]{1,0:T(8,128)(2,1)S(1)}, u32[]{:S(2)}, u32[]{:S(2)}) collective-permute-start(bf16[640,128]{1,0:T(8,128)(2,1)S(1)} %add_convert_fusion.1), channel_id=1, source_target_pairs={{0,2},{1,3},{2,0},{3,1},{4,6},{5,7},{6,4},{7,5},{8,10},{9,11},{10,... | collective-permute-start | bytes 491528 | tf_op jit(solution)/shard_map/ppermute | solution.py:527

commit v2 on v0

--- a/solution.py
+++ b/solution.py
@@ -41,7 +41,7 @@
 def list_chunks(chunks, low_ref, high_ref, own_columns, outer, chunk_list):
     def step(i, counts):
         inner_count, outer_count = counts
-        halo = (low_ref[i] < HALO) | (high_ref[i] >= HALO + own_columns)
+        halo = (low_ref[i, 0] < HALO) | (high_ref[i, 0] >= HALO + own_columns)
         early = jnp.logical_not(halo) & (inner_count < LIMIT)
         count = outer_count if outer else inner_count
 
@@ -67,8 +67,8 @@
             i = chunk_list[t]
             here = lax.shift_right_logical(first_chunk + i, 2) == slot0 + slot
             return (
-                jnp.where(here, jnp.minimum(low, low_ref[i]), low),
-                jnp.where(here, jnp.maximum(high, high_ref[i]), high),
+                jnp.where(here, jnp.minimum(low, low_ref[i, 0]), low),
+                jnp.where(here, jnp.maximum(high, high_ref[i, 0]), high),
             )
 
         low, high = lax.fori_loop(0, count, step, (jnp.int32(1000), jnp.int32(-1)))
@@ -326,6 +326,8 @@
     ]
     for copy in copies:
         copy.start()
+    lows = []
+    highs = []
     for i in range(chunks):
         rows = pl.ds(pl.multiple_of((k * chunks + i) * 4, 4), 4)
         point = senders[rows, :] - lon * points_own + HALO * LAT
@@ -333,8 +335,12 @@
         point = jnp.where(point >= all_points, point - all_points, point)
         points[i * 4 : i * 4 + 4, :] = point * 4
         ids[i * 4 : i * 4 + 4, :] = (receivers[rows, :] - lon * nodes) * 4
-        for ref, end in ((low_ref, jnp.min(point)), (high_ref, jnp.max(point))):
-            ref[i] = lax.shift_right_logical(lax.shift_right_logical(end, 7) * 13108, 16)
+        lows.append(jnp.min(point, axis=0, keepdims=True))
+        highs.append(jnp.max(point, axis=0, keepdims=True))
+    for ref, ends, reduce in ((low_ref, lows, jnp.min), (high_ref, highs, jnp.max)):
+        ends = jnp.concatenate(ends + [ends[0]] * (16 - chunks), axis=0)
+        ends = jnp.broadcast_to(reduce(ends, axis=1, keepdims=True), (16, 128))
+        ref[...] = lax.shift_right_logical(lax.shift_right_logical(ends, 7) * 13108, 16)
     for copy in copies:
         copy.wait()
 
@@ -352,13 +358,13 @@
 def pack_call(chunks, points_own, all_points, channels, nodes, operands):
     half = HALO * LAT // 2
     index = jax.ShapeDtypeStruct((chunks * 4, 128), jnp.int32)
-    ends = jax.ShapeDtypeStruct((chunks,), jnp.int32)
+    ends = jax.ShapeDtypeStruct((16, 128), jnp.int32)
     side = jax.ShapeDtypeStruct((channels, half), bf16)
     return pl.pallas_call(
         functools.partial(pack_kernel, chunks, points_own, all_points, nodes),
         out_shape=(index, index, ends, ends, side, side),
         in_specs=[SMEM] * 2 + [VMEM] * 2 + [ANY],
-        out_specs=(VMEM, VMEM, SMEM, SMEM, VMEM, VMEM),
+        out_specs=(VMEM,) * 6,
         scratch_shapes=[pltpu.SemaphoreType.DMA((2,))],
         name="pack",
     )(*operands)

time: 107 us -> 107 us (level)
  no operation moved by 1% of the time
where the time goes in v2:
time: 107 us
  Pallas kernels  44.6 us (42%)
  waiting for transfers between devices  41 us (38%)
  starting transfers between devices  9.62 us (9%)
  blocking collectives  7.25 us (7%)
  other arithmetic  3.2 us (3%)
    pallas_call x2, Pallas kernels, block_call(): pl.pallas_call(functools.partial(block_kernel, outer, chunks, own_columns...  38.7 us
    ppermute x1, waiting for transfers between devices, encoder(): low_own = lax.ppermute(low_half, 'lon', forward)  12.4 us
    ppermute x1, waiting for transfers between devices, encoder(): mesh_far = lax.ppermute(mesh_latent, 'ch', across)  7.72 us
    ppermute x1, waiting for transfers between devices, encoder(): message_far = lax.ppermute(message_weight, ('lon', 'ch'), facing)  7.49 us
    psum x1, blocking collectives, encoder(): lax.psum((jnp.sum(node_share, axis=1, keepdims=True), jnp.sum(jnp.square(...  7.25 us
    ppermute x1, waiting for transfers between devices, encoder(): far = lax.ppermute(far.astype(bf16), 'ch', across).astype(f32)  6.99 us
    pallas_call x1, Pallas kernels, pack_call(): pl.pallas_call(functools.partial(pack_kernel, chunks, points_own, all_poi...  4.12 us
    ppermute x1, waiting for transfers between devices, encoder(): high_own = lax.ppermute(high_half, 'lon', backward)  3.41 us
  transfers between devices with their start and end apart: 16, of which 8 were waited for; matrix products, arithmetic and copies ran while one was open for 1% of the time, Pallas kernels for 22%

profile of v2, /device:TPU:6, one launch (start us, length us, event | category | flops | bytes accessed | tf_op | source)
XLA Modules:
  0.0 106.6 jit_solution(3056688945602676654)
XLA Ops:
  0.0 0.0 copy-start.10
  0.0 0.0 copy-start.2
  0.0 4.1 %pack.1 = (s32[44,128]{1,0:T(8,128)}, s32[44,128]{1,0:T(8,128)}, s32[16,128]{1,0:T(8,128)}, s32[16,128]{1,0:T(8,128)}, bf16[474,1280]{1,0:T(8,128)(2,1)}, /*index=5*/bf16[474,1280]{1,0:T(8,128)(2,1)}) custom-call(s32[1]{0:T(128)} %bitcast.1.lon_ref, s32[1]{0:T(128)} %bitcast.place.refs_0_, s32[176,128]{1,0:T(8,128)} %bitcast.16, s32[176,128]{1,0:T(8,128)} %bitcast.17, ...), custom_call_target="tpu_custom_call" | custom-call | tf_op jit(solution)/shard_map/pack/pallas_call | solution.py:363
  4.1 1.6 %collective-permute-start = (bf16[474,1280]{1,0:T(8,128)(2,1)}, bf16[474,1280]{1,0:T(8,128)(2,1)S(1)}, u32[]{:S(2)}, u32[]{:S(2)}) collective-permute-start(bf16[474,1280]{1,0:T(8,128)(2,1)} %get-tuple-element.19), channel_id=1, source_target_pairs={{0,4},{4,8},{8,12},{12,16},{16,20},{20,24},{24,28},{28,32},{32,36}... | collective-permute-start | bytes 3640328 | tf_op jit(solution)/shard_map/ppermute | solution.py:481
  5.7 0.5 collective-permute-start.2
  6.2 1.8 %weights.1.refs_9_.refs_13_ = bf16[1040,128]{1,0:T(8,128)(2,1)} custom-call(bf16[4,128]{1,0:T(4,128)(2,1)} %feature_weight.1, f32[1,128]{1,0:T(1,128)} %bitcast.21, bf16[512,128]{1,0:T(8,128)(2,1)} %sender_weight.1, bf16[512,128]{1,0:T(8,128)(2,1)} %receiver_weight.1), custom_call_target="tpu_custom_call" | custom-call | tf_op jit(solution)/shard_map/weights/pallas_call | solution.py:349
  8.0 3.0 %collective-permute-start.5 = (bf16[1040,128]{1,0:T(8,128)(2,1)}, bf16[1040,128]{1,0:T(8,128)(2,1)S(1)}, u32[]{:S(2)}, u32[]{:S(2)}) collective-permute-start(bf16[1040,128]{1,0:T(8,128)(2,1)} %weights.1.refs_9_.refs_13_), channel_id=1, source_target_pairs={{0,18},{1,19},{2,16},{3,17},{4,22},{5,23},{6,20},{7,21},{8,26},{9,... | collective-permute-start | bytes 798728 | tf_op jit(solution)/shard_map/ppermute | solution.py:475
  11.0 0.0 copy-done.10
  11.0 0.2 collective-permute-start.11
  11.2 0.0 copy-done.2
  11.3 2.0 %collective-permute-start.8 = (bf16[640,128]{1,0:T(8,128)(2,1)S(1)}, bf16[640,128]{1,0:T(8,128)(2,1)S(1)}, u32[]{:S(2)}, u32[]{:S(2)}) collective-permute-start(bf16[640,128]{1,0:T(8,128)(2,1)S(1)} %copy-done.2), channel_id=1, source_target_pairs={{0,2},{1,3},{2,0},{3,1},{4,6},{5,7},{6,4},{7,5},{8,10},{9,11},{10,... | collective-permute-start | bytes 491528 | tf_op jit(solution)/shard_map/ppermute | solution.py:476
  13.2 7.5 %collective-permute-done.11.refs_23_ = bf16[128,512]{1,0:T(8,128)(2,1)S(1)} collective-permute-done((bf16[128,512]{1,0:T(8,128)(2,1)S(1)}, bf16[128,512]{1,0:T(8,128)(2,1)S(1)}, u32[]{:S(2)}, u32[]{:S(2)}) %collective-permute-start.11) | collective-permute-done | bytes 131104 | tf_op jit(solution)/shard_map/ppermute | solution.py:489
  20.7 0.0 copy-start.11
  20.7 0.0 collective-permute-start.7
  20.7 12.4 %collective-permute-done.refs_4_ = bf16[474,1280]{1,0:T(8,128)(2,1)S(1)} collective-permute-done((bf16[474,1280]{1,0:T(8,128)(2,1)}, bf16[474,1280]{1,0:T(8,128)(2,1)S(1)}, u32[]{:S(2)}, u32[]{:S(2)}) %collective-permute-start) | collective-permute-done | bytes 1213472 | tf_op jit(solution)/shard_map/ppermute | solution.py:481
  33.2 0.0 copy-start
  33.2 0.0 collective-permute-start.1
  33.2 3.4 %collective-permute-done.2.refs_6_ = bf16[474,1280]{1,0:T(8,128)(2,1)S(1)} collective-permute-done((bf16[474,1280]{1,0:T(8,128)(2,1)}, bf16[474,1280]{1,0:T(8,128)(2,1)S(1)}, u32[]{:S(2)}, u32[]{:S(2)}) %collective-permute-start.2) | collective-permute-done | bytes 1213472 | tf_op jit(solution)/shard_map/ppermute | solution.py:482
  36.6 0.0 copy-start.1
  36.6 0.0 collective-permute-start.3
  36.6 7.7 %collective-permute-done.8.refs_15_.refs_19_ = bf16[640,128]{1,0:T(8,128)(2,1)S(1)} collective-permute-done((bf16[640,128]{1,0:T(8,128)(2,1)S(1)}, bf16[640,128]{1,0:T(8,128)(2,1)S(1)}, u32[]{:S(2)}, u32[]{:S(2)}) %collective-permute-start.8) | collective-permute-done | bytes 163872 | tf_op jit(solution)/shard_map/ppermute | solution.py:476
  44.3 0.0 copy-start.7
  44.3 0.0 collective-permute-start.4
  44.3 0.0 collective-permute-done.5.refs_11_.refs_15_
  44.3 0.0 copy-start.4
  44.3 0.5 collective-permute-start.6
  44.8 0.0 collective-permute-done.7.refs_14_.refs_18_
  44.8 0.1 collective-permute-start.9
  44.9 1.1 %collective-permute-done.4.refs_10_.refs_14_ = bf16[1040,128]{1,0:T(8,128)(2,1)S(1)} collective-permute-done((bf16[1040,128]{1,0:T(8,128)(2,1)}, bf16[1040,128]{1,0:T(8,128)(2,1)S(1)}, u32[]{:S(2)}, u32[]{:S(2)}) %collective-permute-start.4) | collective-permute-done | bytes 266272 | tf_op jit(solution)/shard_map/ppermute | solution.py:485
  46.1 0.1 collective-permute-start.10
  46.2 0.5 collective-permute-done.9.refs_16_.refs_20_
  46.7 0.1 collective-permute-start.12
  46.8 0.0 collective-permute-done.6.refs_12_.refs_16_
  46.8 0.0 copy-done.7
  46.8 0.0 copy-done.4
  46.8 0.0 copy-done.8
  46.9 0.0 copy-done.5
  46.9 0.5 copy-done.9
  47.4 0.2 copy-done.6
  47.6 21.8 %block_inner.1 = (f32[640,512]{1,0:T(8,128)}, f32[640,128]{1,0:T(8,128)}) custom-call(s32[1]{0:T(128)} %bitcast.place.refs_0_, s32[16,128]{1,0:T(8,128)} %get-tuple-element.17.refs_1_, s32[16,128]{1,0:T(8,128)} %get-tuple-element.18.refs_2_, bf16[474,28800]{1,0:T(8,128)(2,1)} %bitcast.12, s32[44,128]{1,0:T(8,128)} %get-tuple-element.21.refs_4_.refs_8_, ...), custom_call_target="tpu_custom_call" | custom-call | flops 9596567552 | bytes 5767168 | tf_op jit(solution)/shard_map/block_inner/pallas_call | solution.py:391
  69.3 0.0 copy-done.11
  69.4 0.0 copy-done
  69.4 0.0 copy-done.1
  69.4 0.0 collective-permute-done.10.refs_22_
  69.4 0.0 collective-permute-done.12.refs_24_
  69.4 0.0 collective-permute-done.1.refs_5_
  69.4 0.0 collective-permute-done.3.refs_7_
  69.4 16.9 %block_outer.1 = (f32[640,128]{1,0:T(8,128)}, f32[640,128]{1,0:T(8,128)}, f32[640,128]{1,0:T(8,128)}, f32[640,128]{1,0:T(8,128)}) custom-call(s32[1]{0:T(128)} %bitcast.place.refs_0_, s32[16,128]{1,0:T(8,128)} %get-tuple-element.17.refs_1_, s32[16,128]{1,0:T(8,128)} %get-tuple-element.18.refs_2_, bf16[474,28800]{1,0:T(8,128)(2,1)} %bitcast.13, ...), custom_call_target="tpu_custom_call" | custom-call | flops 9596567552 | bytes 5767168 | tf_op jit(solution)/shard_map/block_outer/pallas_call | solution.py:391
  86.3 0.0 copy-start.3
  86.3 0.0 copy-start.12
  86.4 0.0 copy-start.13
  86.4 0.1 collective-permute-start.14
  86.5 0.4 collective-permute-start.13
  87.0 1.3 %collective-permute-done.14 = f32[640,128]{1,0:T(8,128)S(1)} collective-permute-done((f32[640,128]{1,0:T(8,128)}, f32[640,128]{1,0:T(8,128)S(1)}, u32[]{:S(2)}, u32[]{:S(2)}) %collective-permute-start.14) | collective-permute-done | bytes 327712 | tf_op jit(solution)/shard_map/ppermute | solution.py:514
  88.3 1.0 add_convert_fusion.1
  89.3 0.8 collective-permute-start.15
  90.2 0.0 collective-permute-done.13
  90.2 7.0 %collective-permute-done.15 = bf16[640,128]{1,0:T(8,128)(2,1)S(1)} collective-permute-done((bf16[640,128]{1,0:T(8,128)(2,1)S(1)}, bf16[640,128]{1,0:T(8,128)(2,1)S(1)}, u32[]{:S(2)}, u32[]{:S(2)}) %collective-permute-start.15) | collective-permute-done | bytes 163872 | tf_op jit(solution)/shard_map/ppermute | solution.py:515
  97.1 1.2 %fusion = (f32[640]{0:T(1024)S(1)}, f32[640]{0:T(1024)S(1)}, f32[640,128]{1,0:T(8,128)S(1)}) fusion(bf16[640,128]{1,0:T(8,128)(2,1)S(1)} %collective-permute-done.15, f32[640,128]{1,0:T(8,128)} %get-tuple-element.25, f32[640,128]{1,0:T(8,128)S(1)} %collective-permute-done.13), kind=kLoop, calls=%fused_computation.6 | loop fusion | flops 490240 | bytes 1152000 | tf_op jit(solution)/shard_map/reduce_sum | solution.py:519
  98.4 7.2 %all-reduce = (f32[640,1]{0,1:T(1,128)S(1)}, f32[640,1]{0,1:T(1,128)S(1)}) all-reduce(f32[640,1]{0,1:T(1,128)S(1)} %broadcast_in_dim.28, f32[640,1]{0,1:T(1,128)S(1)} %broadcast_in_dim.29), channel_id=1, replica_groups=mesh['lon'=32,'ch'=4] {'ch'}, use_global_device_ids=true, to_apply=%region_1.0 | all-reduce | flops 1280 | bytes 10240 | tf_op jit(solution)/shard_map/psum | solution.py:517
  105.7 0.0 copy-done.3
  105.7 0.0 copy-done.12
  105.7 0.0 copy-done.13
  105.7 0.9 add_convert_fusion
  (7 shorter events, 0.0 us)
Async XLA Ops:
  0.0 11.0 %copy-start.10 = (bf16[128,512]{1,0:T(8,128)(2,1)S(1)}, bf16[128,512]{1,0:T(8,128)(2,1)}, u32[]{:S(2)}) copy-start(bf16[128,512]{1,0:T(8,128)(2,1)} %refs_21_.1) | copy-start | bytes 393220
  0.0 11.2 %copy-start.2 = (bf16[640,128]{1,0:T(8,128)(2,1)S(1)}, bf16[640,128]{1,0:T(8,128)(2,1)}, u32[]{:S(2)}) copy-start(bf16[640,128]{1,0:T(8,128)(2,1)} %refs_17_.1) | copy-start | bytes 491524
  4.1 29.0 %collective-permute-start = (bf16[474,1280]{1,0:T(8,128)(2,1)}, bf16[474,1280]{1,0:T(8,128)(2,1)S(1)}, u32[]{:S(2)}, u32[]{:S(2)}) collective-permute-start(bf16[474,1280]{1,0:T(8,128)(2,1)} %get-tuple-element.19), channel_id=1, source_target_pairs={{0,4},{4,8},{8,12},{12,16},{16,20},{20,24},{24,28},{28,32},{32,36}... | collective-permute-start | bytes 3640328 | tf_op jit(solution)/shard_map/ppermute | solution.py:481
  5.7 30.9 %collective-permute-start.2 = (bf16[474,1280]{1,0:T(8,128)(2,1)}, bf16[474,1280]{1,0:T(8,128)(2,1)S(1)}, u32[]{:S(2)}, u32[]{:S(2)}) collective-permute-start(bf16[474,1280]{1,0:T(8,128)(2,1)} %get-tuple-element.20), channel_id=1, source_target_pairs={{4,0},{8,4},{12,8},{16,12},{20,16},{24,20},{28,24},{32,28},{36,32}... | collective-permute-start | bytes 3640328 | tf_op jit(solution)/shard_map/ppermute | solution.py:482
  8.0 36.3 %collective-permute-start.5 = (bf16[1040,128]{1,0:T(8,128)(2,1)}, bf16[1040,128]{1,0:T(8,128)(2,1)S(1)}, u32[]{:S(2)}, u32[]{:S(2)}) collective-permute-start(bf16[1040,128]{1,0:T(8,128)(2,1)} %weights.1.refs_9_.refs_13_), channel_id=1, source_target_pairs={{0,18},{1,19},{2,16},{3,17},{4,22},{5,23},{6,20},{7,21},{8,26},{9,... | collective-permute-start | bytes 798728 | tf_op jit(solution)/shard_map/ppermute | solution.py:475
  11.0 9.7 %collective-permute-start.11 = (bf16[128,512]{1,0:T(8,128)(2,1)S(1)}, bf16[128,512]{1,0:T(8,128)(2,1)S(1)}, u32[]{:S(2)}, u32[]{:S(2)}) collective-permute-start(bf16[128,512]{1,0:T(8,128)(2,1)S(1)} %copy-done.10), channel_id=1, source_target_pairs={{0,18},{1,19},{2,16},{3,17},{4,22},{5,23},{6,20},{7,21},{8,26},{9,... | collective-permute-start | bytes 393224 | tf_op jit(solution)/shard_map/ppermute | solution.py:489
  11.3 33.1 %collective-permute-start.8 = (bf16[640,128]{1,0:T(8,128)(2,1)S(1)}, bf16[640,128]{1,0:T(8,128)(2,1)S(1)}, u32[]{:S(2)}, u32[]{:S(2)}) collective-permute-start(bf16[640,128]{1,0:T(8,128)(2,1)S(1)} %copy-done.2), channel_id=1, source_target_pairs={{0,2},{1,3},{2,0},{3,1},{4,6},{5,7},{6,4},{7,5},{8,10},{9,11},{10,... | collective-permute-start | bytes 491528 | tf_op jit(solution)/shard_map/ppermute | solution.py:476
  20.7 48.6 %copy-start.11 = (bf16[128,512]{1,0:T(8,128)(2,1)}, bf16[128,512]{1,0:T(8,128)(2,1)S(1)}, u32[]{:S(2)}) copy-start(bf16[128,512]{1,0:T(8,128)(2,1)S(1)} %collective-permute-done.11.refs_23_) | copy-start | bytes 393220
  20.7 24.1 %collective-permute-start.7 = (bf16[640,128]{1,0:T(8,128)(2,1)S(1)}, bf16[640,128]{1,0:T(8,128)(2,1)S(1)}, u32[]{:S(2)}, u32[]{:S(2)}) collective-permute-start(bf16[640,128]{1,0:T(8,128)(2,1)S(1)} %copy-done.2), channel_id=1, source_target_pairs={{0,1},{1,0},{2,3},{3,2},{4,5},{5,4},{6,7},{7,6},{8,9},{9,8},{10,11... | collective-permute-start | bytes 491528 | tf_op jit(solution)/shard_map/ppermute | solution.py:487
  33.2 36.2 %copy-start = (bf16[474,1280]{1,0:T(8,128)(2,1)}, bf16[474,1280]{1,0:T(8,128)(2,1)S(1)}, u32[]{:S(2)}) copy-start(bf16[474,1280]{1,0:T(8,128)(2,1)S(1)} %collective-permute-done.refs_4_) | copy-start | bytes 3640324
  33.2 36.2 %collective-permute-start.1 = (bf16[474,1280]{1,0:T(8,128)(2,1)S(1)}, bf16[474,1280]{1,0:T(8,128)(2,1)}, u32[]{:S(2)}, u32[]{:S(2)}) collective-permute-start(bf16[474,1280]{1,0:T(8,128)(2,1)S(1)} %collective-permute-done.refs_4_), channel_id=1, source_target_pairs={{0,1},{1,0},{2,3},{3,2},{4,5},{5,4},{6,7},{7,6},{8,9},{9,8},{10,11... | collective-permute-start | bytes 3640328 | tf_op jit(solution)/shard_map/ppermute | solution.py:483
  36.6 32.8 %copy-start.1 = (bf16[474,1280]{1,0:T(8,128)(2,1)}, bf16[474,1280]{1,0:T(8,128)(2,1)S(1)}, u32[]{:S(2)}) copy-start(bf16[474,1280]{1,0:T(8,128)(2,1)S(1)} %collective-permute-done.2.refs_6_) | copy-start | bytes 3640324
  36.6 32.8 %collective-permute-start.3 = (bf16[474,1280]{1,0:T(8,128)(2,1)S(1)}, bf16[474,1280]{1,0:T(8,128)(2,1)}, u32[]{:S(2)}, u32[]{:S(2)}) collective-permute-start(bf16[474,1280]{1,0:T(8,128)(2,1)S(1)} %collective-permute-done.2.refs_6_), channel_id=1, source_target_pairs={{0,1},{1,0},{2,3},{3,2},{4,5},{5,4},{6,7},{7,6},{8,9},{9,8},{10,11... | collective-permute-start | bytes 3640328 | tf_op jit(solution)/shard_map/ppermute | solution.py:484
  44.3 2.5 %copy-start.7 = (bf16[640,128]{1,0:T(8,128)(2,1)}, bf16[640,128]{1,0:T(8,128)(2,1)S(1)}, u32[]{:S(2)}) copy-start(bf16[640,128]{1,0:T(8,128)(2,1)S(1)} %collective-permute-done.8.refs_15_.refs_19_) | copy-start | bytes 491524
  44.3 1.8 %collective-permute-start.4 = (bf16[1040,128]{1,0:T(8,128)(2,1)}, bf16[1040,128]{1,0:T(8,128)(2,1)S(1)}, u32[]{:S(2)}, u32[]{:S(2)}) collective-permute-start(bf16[1040,128]{1,0:T(8,128)(2,1)} %weights.1.refs_9_.refs_13_), channel_id=1, source_target_pairs={{0,1},{1,0},{2,3},{3,2},{4,5},{5,4},{6,7},{7,6},{8,9},{9,8},{10,11... | collective-permute-start | bytes 798728 | tf_op jit(solution)/shard_map/ppermute | solution.py:485
  44.3 2.5 %copy-start.4 = (bf16[1040,128]{1,0:T(8,128)(2,1)}, bf16[1040,128]{1,0:T(8,128)(2,1)S(1)}, u32[]{:S(2)}) copy-start(bf16[1040,128]{1,0:T(8,128)(2,1)S(1)} %collective-permute-done.5.refs_11_.refs_15_) | copy-start | bytes 798724
  44.3 2.5 %collective-permute-start.6 = (bf16[1040,128]{1,0:T(8,128)(2,1)S(1)}, bf16[1040,128]{1,0:T(8,128)(2,1)S(1)}, u32[]{:S(2)}, u32[]{:S(2)}) collective-permute-start(bf16[1040,128]{1,0:T(8,128)(2,1)S(1)} %collective-permute-done.5.refs_11_.refs_15_), channel_id=1, source_target_pairs={{0,1},{1,0},{2,3},{3,2},{4,5},{5,4},{6,7},{7,6},{8,9},{9,8},{10,11... | collective-permute-start | bytes 798728 | tf_op jit(solution)/shard_map/ppermute | solution.py:486
  44.8 2.0 %copy-start.8 = (bf16[640,128]{1,0:T(8,128)(2,1)}, bf16[640,128]{1,0:T(8,128)(2,1)S(1)}, u32[]{:S(2)}) copy-start(bf16[640,128]{1,0:T(8,128)(2,1)S(1)} %collective-permute-done.7.refs_14_.refs_18_) | copy-start | bytes 491524
  44.8 1.8 %collective-permute-start.9 = (bf16[640,128]{1,0:T(8,128)(2,1)S(1)}, bf16[640,128]{1,0:T(8,128)(2,1)S(1)}, u32[]{:S(2)}, u32[]{:S(2)}) collective-permute-start(bf16[640,128]{1,0:T(8,128)(2,1)S(1)} %collective-permute-done.8.refs_15_.refs_19_), channel_id=1, source_target_pairs={{0,1},{1,0},{2,3},{3,2},{4,5},{5,4},{6,7},{7,6},{8,9},{9,8},{10,11... | collective-permute-start | bytes 491528 | tf_op jit(solution)/shard_map/ppermute | solution.py:488
  46.1 0.8 copy-start.5
  46.1 23.3 %collective-permute-start.10 = (bf16[128,512]{1,0:T(8,128)(2,1)S(1)}, bf16[128,512]{1,0:T(8,128)(2,1)}, u32[]{:S(2)}, u32[]{:S(2)}) collective-permute-start(bf16[128,512]{1,0:T(8,128)(2,1)S(1)} %copy-done.10), channel_id=1, source_target_pairs={{0,1},{1,0},{2,3},{3,2},{4,5},{5,4},{6,7},{7,6},{8,9},{9,8},{10,11... | collective-permute-start | bytes 393224 | tf_op jit(solution)/shard_map/ppermute | solution.py:490
  46.7 0.7 copy-start.9
  46.7 22.7 %collective-permute-start.12 = (bf16[128,512]{1,0:T(8,128)(2,1)S(1)}, bf16[128,512]{1,0:T(8,128)(2,1)}, u32[]{:S(2)}, u32[]{:S(2)}) collective-permute-start(bf16[128,512]{1,0:T(8,128)(2,1)S(1)} %collective-permute-done.11.refs_23_), channel_id=1, source_target_pairs={{0,1},{1,0},{2,3},{3,2},{4,5},{5,4},{6,7},{7,6},{8,9},{9,8},{10,11... | collective-permute-start | bytes 393224 | tf_op jit(solution)/shard_map/ppermute | solution.py:491
  46.8 0.7 copy-start.6
  86.3 19.4 %copy-start.3 = (bf16[640,128]{1,0:T(8,128)(2,1)S(1)}, bf16[640,128]{1,0:T(8,128)(2,1)}, u32[]{:S(2)}) copy-start(bf16[640,128]{1,0:T(8,128)(2,1)} %refs_17_.1) | copy-start | bytes 491524
  86.3 19.4 %copy-start.12 = (f32[128]{0:T(128)S(1)}, f32[128]{0:T(128)}, u32[]{:S(2)}) copy-start(f32[128]{0:T(128)} %param.29) | copy-start | bytes 1540
  86.4 19.4 %copy-start.13 = (f32[128]{0:T(128)S(1)}, f32[128]{0:T(128)}, u32[]{:S(2)}) copy-start(f32[128]{0:T(128)} %param.28) | copy-start | bytes 1540
  86.4 1.9 %collective-permute-start.14 = (f32[640,128]{1,0:T(8,128)}, f32[640,128]{1,0:T(8,128)S(1)}, u32[]{:S(2)}, u32[]{:S(2)}) collective-permute-start(f32[640,128]{1,0:T(8,128)} %get-tuple-element.28), channel_id=1, source_target_pairs={{0,1},{1,0},{2,3},{3,2},{4,5},{5,4},{6,7},{7,6},{8,9},{9,8},{10,11... | collective-permute-start | bytes 983048 | tf_op jit(solution)/shard_map/ppermute | solution.py:514
  86.5 3.6 %collective-permute-start.13 = (f32[640,128]{1,0:T(8,128)}, f32[640,128]{1,0:T(8,128)S(1)}, u32[]{:S(2)}, u32[]{:S(2)}) collective-permute-start(f32[640,128]{1,0:T(8,128)} %get-tuple-element.26), channel_id=1, source_target_pairs={{0,1},{1,0},{2,3},{3,2},{4,5},{5,4},{6,7},{7,6},{8,9},{9,8},{10,11... | collective-permute-start | bytes 983048 | tf_op jit(solution)/shard_map/ppermute | solution.py:516
  89.3 7.8 %collective-permute-start.15 = (bf16[640,128]{1,0:T(8,128)(2,1)S(1)}, bf16[640,128]{1,0:T(8,128)(2,1)S(1)}, u32[]{:S(2)}, u32[]{:S(2)}) collective-permute-start(bf16[640,128]{1,0:T(8,128)(2,1)S(1)} %add_convert_fusion.1), channel_id=1, source_target_pairs={{0,2},{1,3},{2,0},{3,1},{4,6},{5,7},{6,4},{7,5},{8,10},{9,11},{10,... | collective-permute-start | bytes 491528 | tf_op jit(solution)/shard_map/ppermute | solution.py:515

commit v3 on v0

--- a/solution.py
+++ b/solution.py
@@ -103,8 +103,6 @@
     meshes = refs[9:13]
     refs = refs[13:]
     if outer:
-        messages = refs[:4]
-        refs = refs[4:]
         message_bias, first_totals, first_tally, *parts = refs[:7]
         totals, tally = refs[-2:]
         refs = refs[7:-2]
@@ -134,11 +132,14 @@
     late = []
     if outer:
         for j in range(4):
-            late.append(
-                pltpu.make_async_copy(
-                    messages[j], message_weight.at[pl.ds(j * 128, 128)], sems.at[16 + j]
+            for q in range(4):
+                late.append(
+                    pltpu.make_async_copy(
+                        bundles[j].at[pl.ds(1040 + q * 128, 128)],
+                        message_weight.at[pl.ds(j * 128, 128), pl.ds(q * 128, 128)],
+                        sems.at[32 + j * 4 + q],
+                    )
                 )
-            )
         for copy in late:
             copy.start()
         totals[...] = first_totals[...]
@@ -296,7 +297,13 @@
         parts[2 + r][...] = totals[:, pl.ds(theirs, 128)]
 
 
-def weights_kernel(feature_weight, hidden_bias, sender_weight, receiver_weight, bundle):
+def weights_kernel(feature_weight, hidden_bias, sender_weight, receiver_weight, message_weight,
+                   bundle):
+    share = message_weight.shape[0]
+    for q in range(4):
+        bundle[1040 + q * share : 1040 + (q + 1) * share, :] = message_weight[
+            :, q * share : (q + 1) * share
+        ]
     bundle[0:512, :] = sender_weight[...]
     bundle[512:1024, :] = receiver_weight[...]
     bias = hidden_bias[...]
@@ -342,8 +349,8 @@
 def weights_call(share, operands):
     return pl.pallas_call(
         weights_kernel,
-        out_shape=jax.ShapeDtypeStruct((1040, share), bf16),
-        in_specs=[VMEM] * 4,
+        out_shape=jax.ShapeDtypeStruct((1552, share), bf16),
+        in_specs=[VMEM] * 5,
         out_specs=VMEM,
         name="weights",
     )(*operands)
@@ -378,7 +385,7 @@
     )
     specs = [SMEM] * 3 + [ANY] * (5 if outer else 1) + [VMEM] * 5 + [ANY] * 8
     if outer:
-        specs = specs + [ANY] * 4 + [VMEM] * 3
+        specs = specs + [VMEM] * 3
     slots = SLOTS * WINDOW
     edges = chunks * CHUNK
     square = pltpu.VMEM((width, width), bf16)
@@ -407,7 +414,7 @@
             pltpu.SMEM((32,), jnp.int32),
             pltpu.SMEM((8,), jnp.int32),
             pltpu.SemaphoreType.DMA((BUFFERS,)),
-            pltpu.SemaphoreType.DMA((32,)),
+            pltpu.SemaphoreType.DMA((48,)),
         ]
         + ([pltpu.VMEM(value.shape, f32) for value in sums] if outer else []),
         compiler_params=pltpu.CompilerParams(vmem_limit_bytes=60 * 2**20),
@@ -464,7 +471,9 @@
     lon_scalar = lon_place[None].astype(jnp.int32)
     bundle = weights_call(
         message_weight.shape[0],
-        [feature_weight, hidden_bias[None, :], sender_weight, receiver_weight],
+        [
+            feature_weight, hidden_bias[None, :], sender_weight, receiver_weight, message_weight,
+        ],
     )
     bundle_far = lax.ppermute(bundle, ("lon", "ch"), facing)
     mesh_far = lax.ppermute(mesh_latent, "ch", across)
@@ -480,9 +489,6 @@
     bundle_last = lax.ppermute(bundle_far, "ch", swap)
     mesh_near = lax.ppermute(mesh_latent, "ch", swap)
     mesh_last = lax.ppermute(mesh_far, "ch", swap)
-    message_far = lax.ppermute(message_weight, ("lon", "ch"), facing)
-    message_near = lax.ppermute(message_weight, "ch", swap)
-    message_last = lax.ppermute(message_far, "ch", swap)
     feature_blocks = jnp.transpose(
         edge_features.reshape(edge_features.shape[0], all_chunks, CHUNK), (1, 0, 2)
     )
@@ -502,7 +508,6 @@
         operands=scalars
         + [low_own, low_swap, high_own, high_swap]
         + arrays
-        + [message_weight, message_near, message_far, message_last]
         + [message_bias[None, :], totals, tally],
     )
     far = keep_far + lax.ppermute(send_far, "ch", swap)

time: 107 us -> 110 us (1.028)
  waiting for transfers between devices: 41 us -> 46 us
  starting transfers between devices: 9.66 us -> 7.15 us
    ppermute x1, waiting for transfers between devices: 7.72 us -> 23.5 us  [encoder(): mesh_far = lax.ppermute(mesh_latent, 'ch', across)]
    ppermute x1, waiting for transfers between devices: 12.4 us -> 0.01 us  [encoder(): low_own = lax.ppermute(low_half, 'lon', forward)]
    ppermute x1, waiting for transfers between devices: 0.01 us -> 9.06 us  [encoder(): bundle_far = lax.ppermute(bundle, ('lon', 'ch'), facing)]
    ppermute x3 -> x0, waiting for transfers between devices: 7.49 us -> none  [the longest x1 7.49 us: encoder(): message_far = lax.ppermute(message_weight, ('lon', 'ch'), facing)]
    ppermute x1, waiting for transfers between devices: 3.41 us -> 0.01 us  [encoder(): high_own = lax.ppermute(high_half, 'lon', backward)]
    ppermute x1, waiting for transfers between devices: 0.48 us -> 3.6 us  [encoder(): mesh_last = lax.ppermute(mesh_far, 'ch', swap)]
    ppermute x1, starting transfers between devices: 1.98 us -> 0.63 us  [encoder(): mesh_far = lax.ppermute(mesh_latent, 'ch', across)]
    ppermute x1, waiting for transfers between devices: 1.13 us -> 0.01 us  [encoder(): bundle_near = lax.ppermute(bundle, 'ch', swap)]
  transfers between devices with their start and end apart: 16 -> 13, of which waited for: 8 -> 6; matrix products, arithmetic and copies ran while one was open for 1% -> 1% of each run, Pallas kernels for 22% -> 22%
where the time goes in v3:
time: 110 us
  waiting for transfers between devices  46 us (42%)
  Pallas kernels  45 us (41%)
  blocking collectives  7.34 us (7%)
  starting transfers between devices  7.15 us (6%)
  other arithmetic  3.2 us (3%)
    pallas_call x2, Pallas kernels, block_call(): pl.pallas_call(functools.partial(block_kernel, outer, chunks, own_columns...  39 us
    ppermute x1, waiting for transfers between devices, encoder(): mesh_far = lax.ppermute(mesh_latent, 'ch', across)  23.5 us
    ppermute x1, waiting for transfers between devices, encoder(): bundle_far = lax.ppermute(bundle, ('lon', 'ch'), facing)  9.06 us
    ppermute x1, waiting for transfers between devices, encoder(): far = lax.ppermute(far.astype(bf16), 'ch', across).astype(f32)  7.72 us
    psum x1, blocking collectives, encoder(): lax.psum((jnp.sum(node_share, axis=1, keepdims=True), jnp.sum(jnp.square(...  7.34 us
    pallas_call x1, Pallas kernels, pack_call(): pl.pallas_call(functools.partial(pack_kernel, chunks, points_own, all_poi...  4.12 us
    ppermute x1, waiting for transfers between devices, encoder(): mesh_last = lax.ppermute(mesh_far, 'ch', swap)  3.6 us
    ppermute x1, starting transfers between devices, encoder(): bundle_far = lax.ppermute(bundle, ('lon', 'ch'), facing)  3.01 us
  transfers between devices with their start and end apart: 13, of which 6 were waited for; matrix products, arithmetic and copies ran while one was open for 1% of the time, Pallas kernels for 22%

profile of v3, /device:TPU:6, one launch (start us, length us, event | category | flops | bytes accessed | tf_op | source)
XLA Modules:
  0.0 109.9 jit_solution(16789143513217378865)
XLA Ops:
  0.0 0.0 copy-start.2
  0.0 4.1 %pack.1 = (s32[44,128]{1,0:T(8,128)}, s32[44,128]{1,0:T(8,128)}, s32[11]{0:T(128)}, s32[11]{0:T(128)}, bf16[474,1280]{1,0:T(8,128)(2,1)}, /*index=5*/bf16[474,1280]{1,0:T(8,128)(2,1)}) custom-call(s32[1]{0:T(128)} %bitcast.1.lon_ref, s32[1]{0:T(128)} %bitcast.place.refs_0_, s32[176,128]{1,0:T(8,128)} %bitcast.16, s32[176,128]{1,0:T(8,128)} %bitcast.17, ...), custom_call_target="tpu_custom_call" | custom-call | tf_op jit(solution)/shard_map/pack/pallas_call | solution.py:364
  4.1 1.6 %collective-permute-start = (bf16[474,1280]{1,0:T(8,128)(2,1)}, bf16[474,1280]{1,0:T(8,128)(2,1)S(1)}, u32[]{:S(2)}, u32[]{:S(2)}) collective-permute-start(bf16[474,1280]{1,0:T(8,128)(2,1)} %get-tuple-element.19), channel_id=1, source_target_pairs={{0,4},{4,8},{8,12},{12,16},{16,20},{20,24},{24,28},{28,32},{32,36}... | collective-permute-start | bytes 3640328 | tf_op jit(solution)/shard_map/ppermute | solution.py:484
  5.7 0.5 collective-permute-start.2
  6.2 1.9 %weights.1.refs_9_.refs_13_ = bf16[1552,128]{1,0:T(8,128)(2,1)} custom-call(bf16[4,128]{1,0:T(4,128)(2,1)} %feature_weight.1, f32[1,128]{1,0:T(1,128)} %bitcast.21, bf16[512,128]{1,0:T(8,128)(2,1)} %sender_weight.1, bf16[512,128]{1,0:T(8,128)(2,1)} %receiver_weight.1, bf16[128,512]{1,0:T(8,128)(2,1)} %message_weight.1), custom_call_target="tpu_custom_call" | custom-call | tf_op jit(solution)/shard_map/weights/pallas_call | solution.py:350
  8.1 3.0 %collective-permute-start.5 = (bf16[1552,128]{1,0:T(8,128)(2,1)}, bf16[1552,128]{1,0:T(8,128)(2,1)S(1)}, u32[]{:S(2)}, u32[]{:S(2)}) collective-permute-start(bf16[1552,128]{1,0:T(8,128)(2,1)} %weights.1.refs_9_.refs_13_), channel_id=1, source_target_pairs={{0,18},{1,19},{2,16},{3,17},{4,22},{5,23},{6,20},{7,21},{8,26},{9,... | collective-permute-start | bytes 1191944 | tf_op jit(solution)/shard_map/ppermute | solution.py:478
  11.1 0.0 copy-done.2
  11.1 0.6 collective-permute-start.8
  11.8 0.0 collective-permute-start.4
  11.8 9.1 %collective-permute-done.5.refs_11_.refs_15_ = bf16[1552,128]{1,0:T(8,128)(2,1)S(1)} collective-permute-done((bf16[1552,128]{1,0:T(8,128)(2,1)}, bf16[1552,128]{1,0:T(8,128)(2,1)S(1)}, u32[]{:S(2)}, u32[]{:S(2)}) %collective-permute-start.5) | collective-permute-done | bytes 397344 | tf_op jit(solution)/shard_map/ppermute | solution.py:478
  20.8 0.0 copy-start.4
  20.8 0.0 collective-permute-start.6
  20.8 23.5 %collective-permute-done.8.refs_15_.refs_19_ = bf16[640,128]{1,0:T(8,128)(2,1)S(1)} collective-permute-done((bf16[640,128]{1,0:T(8,128)(2,1)S(1)}, bf16[640,128]{1,0:T(8,128)(2,1)S(1)}, u32[]{:S(2)}, u32[]{:S(2)}) %collective-permute-start.8) | collective-permute-done | bytes 163872 | tf_op jit(solution)/shard_map/ppermute | solution.py:479
  44.3 0.0 copy-start.7
  44.3 0.0 collective-permute-start.7
  44.3 0.0 collective-permute-done.refs_4_
  44.3 0.0 copy-start
  44.3 0.5 collective-permute-start.1
  44.8 0.0 collective-permute-done.2.refs_6_
  44.9 0.0 copy-start.1
  44.9 0.1 collective-permute-start.3
  45.0 0.8 collective-permute-done.7.refs_14_.refs_18_
  45.7 0.0 copy-start.8
  45.7 0.1 collective-permute-start.9
  45.9 3.6 %collective-permute-done.9.refs_16_.refs_20_ = bf16[640,128]{1,0:T(8,128)(2,1)S(1)} collective-permute-done((bf16[640,128]{1,0:T(8,128)(2,1)S(1)}, bf16[640,128]{1,0:T(8,128)(2,1)S(1)}, u32[]{:S(2)}, u32[]{:S(2)}) %collective-permute-start.9) | collective-permute-done | bytes 163872 | tf_op jit(solution)/shard_map/ppermute | solution.py:491
  49.5 0.0 copy-start.9
  49.5 0.0 collective-permute-done.4.refs_10_.refs_14_
  49.5 0.0 copy-start.5
  49.5 0.0 collective-permute-done.6.refs_12_.refs_16_
  49.5 0.0 copy-done.8
  49.5 0.0 copy-start.6
  49.5 0.0 copy-done.4
  49.5 0.0 copy-done.7
  49.5 0.6 copy-done.9
  50.1 0.2 copy-done.5
  50.3 0.1 copy-done.6
  50.4 21.9 %block_inner.1 = (f32[640,512]{1,0:T(8,128)}, f32[640,128]{1,0:T(8,128)}) custom-call(s32[1]{0:T(128)} %bitcast.place.refs_0_, s32[11]{0:T(128)} %get-tuple-element.17.refs_1_, s32[11]{0:T(128)} %get-tuple-element.18.refs_2_, bf16[474,28800]{1,0:T(8,128)(2,1)} %bitcast.12, s32[44,128]{1,0:T(8,128)} %get-tuple-element.21.refs_4_.refs_8_, ...), custom_call_target="tpu_custom_call" | custom-call | flops 9596567552 | bytes 5767168 | tf_op jit(solution)/shard_map/block_inner/pallas_call | solution.py:392
  72.3 0.0 copy-done
  72.3 0.0 copy-done.1
  72.3 0.0 collective-permute-done.1.refs_5_
  72.3 0.0 collective-permute-done.3.refs_7_
  72.3 17.1 %block_outer.1 = (f32[640,128]{1,0:T(8,128)}, f32[640,128]{1,0:T(8,128)}, f32[640,128]{1,0:T(8,128)}, f32[640,128]{1,0:T(8,128)}) custom-call(s32[1]{0:T(128)} %bitcast.place.refs_0_, s32[11]{0:T(128)} %get-tuple-element.17.refs_1_, s32[11]{0:T(128)} %get-tuple-element.18.refs_2_, bf16[474,28800]{1,0:T(8,128)(2,1)} %bitcast.13, bf16[474,1280]{1,0:T(8,128)(2,1)} %copy-done, ...), custom_call_target="tpu_custom_call" | custom-call | flops 9596567552 | bytes 5767168 | tf_op jit(solution)/shard_map/block_outer/pallas_call | solution.py:392
  89.5 0.0 copy-start.3
  89.5 0.0 copy-start.10
  89.5 0.0 copy-start.11
  89.5 0.1 collective-permute-start.11
  89.6 0.5 collective-permute-start.10
  90.1 1.3 %collective-permute-done.11 = f32[640,128]{1,0:T(8,128)S(1)} collective-permute-done((f32[640,128]{1,0:T(8,128)}, f32[640,128]{1,0:T(8,128)S(1)}, u32[]{:S(2)}, u32[]{:S(2)}) %collective-permute-start.11) | collective-permute-done | bytes 327712 | tf_op jit(solution)/shard_map/ppermute | solution.py:513
  91.4 1.0 add_convert_fusion.1
  92.4 0.1 collective-permute-start.12
  92.5 0.0 collective-permute-done.10
  92.5 7.7 %collective-permute-done.12 = bf16[640,128]{1,0:T(8,128)(2,1)S(1)} collective-permute-done((bf16[640,128]{1,0:T(8,128)(2,1)S(1)}, bf16[640,128]{1,0:T(8,128)(2,1)S(1)}, u32[]{:S(2)}, u32[]{:S(2)}) %collective-permute-start.12) | collective-permute-done | bytes 163872 | tf_op jit(solution)/shard_map/ppermute | solution.py:514
  100.3 1.2 %fusion = (f32[640]{0:T(1024)S(1)}, f32[640]{0:T(1024)S(1)}, f32[640,128]{1,0:T(8,128)S(1)}) fusion(bf16[640,128]{1,0:T(8,128)(2,1)S(1)} %collective-permute-done.12, f32[640,128]{1,0:T(8,128)} %get-tuple-element.25, f32[640,128]{1,0:T(8,128)S(1)} %collective-permute-done.10), kind=kLoop, calls=%fused_computation.6 | loop fusion | flops 490240 | bytes 1152000 | tf_op jit(solution)/shard_map/reduce_sum | solution.py:518
  101.5 7.3 %all-reduce = (f32[640,1]{0,1:T(1,128)S(1)}, f32[640,1]{0,1:T(1,128)S(1)}) all-reduce(f32[640,1]{0,1:T(1,128)S(1)} %broadcast_in_dim.28, f32[640,1]{0,1:T(1,128)S(1)} %broadcast_in_dim.29), channel_id=1, replica_groups=mesh['lon'=32,'ch'=4] {'ch'}, use_global_device_ids=true, to_apply=%region_1.0 | all-reduce | flops 1280 | bytes 10240 | tf_op jit(solution)/shard_map/psum | solution.py:516
  108.9 0.0 copy-done.3
  108.9 0.0 copy-done.10
  108.9 0.0 copy-done.11
  108.9 0.9 add_convert_fusion
  (3 shorter events, 0.0 us)
Async XLA Ops:
  0.0 11.1 %copy-start.2 = (bf16[640,128]{1,0:T(8,128)(2,1)S(1)}, bf16[640,128]{1,0:T(8,128)(2,1)}, u32[]{:S(2)}) copy-start(bf16[640,128]{1,0:T(8,128)(2,1)} %refs_17_.1) | copy-start | bytes 491524
  4.1 40.2 %collective-permute-start = (bf16[474,1280]{1,0:T(8,128)(2,1)}, bf16[474,1280]{1,0:T(8,128)(2,1)S(1)}, u32[]{:S(2)}, u32[]{:S(2)}) collective-permute-start(bf16[474,1280]{1,0:T(8,128)(2,1)} %get-tuple-element.19), channel_id=1, source_target_pairs={{0,4},{4,8},{8,12},{12,16},{16,20},{20,24},{24,28},{28,32},{32,36}... | collective-permute-start | bytes 3640328 | tf_op jit(solution)/shard_map/ppermute | solution.py:484
  5.7 39.2 %collective-permute-start.2 = (bf16[474,1280]{1,0:T(8,128)(2,1)}, bf16[474,1280]{1,0:T(8,128)(2,1)S(1)}, u32[]{:S(2)}, u32[]{:S(2)}) collective-permute-start(bf16[474,1280]{1,0:T(8,128)(2,1)} %get-tuple-element.20), channel_id=1, source_target_pairs={{4,0},{8,4},{12,8},{16,12},{20,16},{24,20},{28,24},{32,28},{36,32}... | collective-permute-start | bytes 3640328 | tf_op jit(solution)/shard_map/ppermute | solution.py:485
  8.1 12.7 %collective-permute-start.5 = (bf16[1552,128]{1,0:T(8,128)(2,1)}, bf16[1552,128]{1,0:T(8,128)(2,1)S(1)}, u32[]{:S(2)}, u32[]{:S(2)}) collective-permute-start(bf16[1552,128]{1,0:T(8,128)(2,1)} %weights.1.refs_9_.refs_13_), channel_id=1, source_target_pairs={{0,18},{1,19},{2,16},{3,17},{4,22},{5,23},{6,20},{7,21},{8,26},{9,... | collective-permute-start | bytes 1191944 | tf_op jit(solution)/shard_map/ppermute | solution.py:478
  11.1 33.2 %collective-permute-start.8 = (bf16[640,128]{1,0:T(8,128)(2,1)S(1)}, bf16[640,128]{1,0:T(8,128)(2,1)S(1)}, u32[]{:S(2)}, u32[]{:S(2)}) collective-permute-start(bf16[640,128]{1,0:T(8,128)(2,1)S(1)} %copy-done.2), channel_id=1, source_target_pairs={{0,2},{1,3},{2,0},{3,1},{4,6},{5,7},{6,4},{7,5},{8,10},{9,11},{10,... | collective-permute-start | bytes 491528 | tf_op jit(solution)/shard_map/ppermute | solution.py:479
  11.8 37.7 %collective-permute-start.4 = (bf16[1552,128]{1,0:T(8,128)(2,1)}, bf16[1552,128]{1,0:T(8,128)(2,1)S(1)}, u32[]{:S(2)}, u32[]{:S(2)}) collective-permute-start(bf16[1552,128]{1,0:T(8,128)(2,1)} %weights.1.refs_9_.refs_13_), channel_id=1, source_target_pairs={{0,1},{1,0},{2,3},{3,2},{4,5},{5,4},{6,7},{7,6},{8,9},{9,8},{10,11... | collective-permute-start | bytes 1191944 | tf_op jit(solution)/shard_map/ppermute | solution.py:488
  20.8 28.7 %copy-start.4 = (bf16[1552,128]{1,0:T(8,128)(2,1)}, bf16[1552,128]{1,0:T(8,128)(2,1)S(1)}, u32[]{:S(2)}) copy-start(bf16[1552,128]{1,0:T(8,128)(2,1)S(1)} %collective-permute-done.5.refs_11_.refs_15_) | copy-start | bytes 1191940
  20.8 28.7 %collective-permute-start.6 = (bf16[1552,128]{1,0:T(8,128)(2,1)S(1)}, bf16[1552,128]{1,0:T(8,128)(2,1)S(1)}, u32[]{:S(2)}, u32[]{:S(2)}) collective-permute-start(bf16[1552,128]{1,0:T(8,128)(2,1)S(1)} %collective-permute-done.5.refs_11_.refs_15_), channel_id=1, source_target_pairs={{0,1},{1,0},{2,3},{3,2},{4,5},{5,4},{6,7},{7,6},{8,9},{9,8},{10,11... | collective-permute-start | bytes 1191944 | tf_op jit(solution)/shard_map/ppermute | solution.py:489
  44.3 5.2 %copy-start.7 = (bf16[640,128]{1,0:T(8,128)(2,1)}, bf16[640,128]{1,0:T(8,128)(2,1)S(1)}, u32[]{:S(2)}) copy-start(bf16[640,128]{1,0:T(8,128)(2,1)S(1)} %collective-permute-done.8.refs_15_.refs_19_) | copy-start | bytes 491524
  44.3 1.4 %collective-permute-start.7 = (bf16[640,128]{1,0:T(8,128)(2,1)S(1)}, bf16[640,128]{1,0:T(8,128)(2,1)S(1)}, u32[]{:S(2)}, u32[]{:S(2)}) collective-permute-start(bf16[640,128]{1,0:T(8,128)(2,1)S(1)} %copy-done.2), channel_id=1, source_target_pairs={{0,1},{1,0},{2,3},{3,2},{4,5},{5,4},{6,7},{7,6},{8,9},{9,8},{10,11... | collective-permute-start | bytes 491528 | tf_op jit(solution)/shard_map/ppermute | solution.py:490
  44.3 28.0 %copy-start = (bf16[474,1280]{1,0:T(8,128)(2,1)}, bf16[474,1280]{1,0:T(8,128)(2,1)S(1)}, u32[]{:S(2)}) copy-start(bf16[474,1280]{1,0:T(8,128)(2,1)S(1)} %collective-permute-done.refs_4_) | copy-start | bytes 3640324
  44.3 28.0 %collective-permute-start.1 = (bf16[474,1280]{1,0:T(8,128)(2,1)S(1)}, bf16[474,1280]{1,0:T(8,128)(2,1)}, u32[]{:S(2)}, u32[]{:S(2)}) collective-permute-start(bf16[474,1280]{1,0:T(8,128)(2,1)S(1)} %collective-permute-done.refs_4_), channel_id=1, source_target_pairs={{0,1},{1,0},{2,3},{3,2},{4,5},{5,4},{6,7},{7,6},{8,9},{9,8},{10,11... | collective-permute-start | bytes 3640328 | tf_op jit(solution)/shard_map/ppermute | solution.py:486
  44.9 27.5 %copy-start.1 = (bf16[474,1280]{1,0:T(8,128)(2,1)}, bf16[474,1280]{1,0:T(8,128)(2,1)S(1)}, u32[]{:S(2)}) copy-start(bf16[474,1280]{1,0:T(8,128)(2,1)S(1)} %collective-permute-done.2.refs_6_) | copy-start | bytes 3640324
  44.9 27.5 %collective-permute-start.3 = (bf16[474,1280]{1,0:T(8,128)(2,1)S(1)}, bf16[474,1280]{1,0:T(8,128)(2,1)}, u32[]{:S(2)}, u32[]{:S(2)}) collective-permute-start(bf16[474,1280]{1,0:T(8,128)(2,1)S(1)} %collective-permute-done.2.refs_6_), channel_id=1, source_target_pairs={{0,1},{1,0},{2,3},{3,2},{4,5},{5,4},{6,7},{7,6},{8,9},{9,8},{10,11... | collective-permute-start | bytes 3640328 | tf_op jit(solution)/shard_map/ppermute | solution.py:487
  45.7 3.8 %copy-start.8 = (bf16[640,128]{1,0:T(8,128)(2,1)}, bf16[640,128]{1,0:T(8,128)(2,1)S(1)}, u32[]{:S(2)}) copy-start(bf16[640,128]{1,0:T(8,128)(2,1)S(1)} %collective-permute-done.7.refs_14_.refs_18_) | copy-start | bytes 491524
  45.7 3.7 %collective-permute-start.9 = (bf16[640,128]{1,0:T(8,128)(2,1)S(1)}, bf16[640,128]{1,0:T(8,128)(2,1)S(1)}, u32[]{:S(2)}, u32[]{:S(2)}) collective-permute-start(bf16[640,128]{1,0:T(8,128)(2,1)S(1)} %collective-permute-done.8.refs_15_.refs_19_), channel_id=1, source_target_pairs={{0,1},{1,0},{2,3},{3,2},{4,5},{5,4},{6,7},{7,6},{8,9},{9,8},{10,11... | collective-permute-start | bytes 491528 | tf_op jit(solution)/shard_map/ppermute | solution.py:491
  49.5 0.7 copy-start.9
  49.5 0.8 copy-start.5
  49.5 0.9 copy-start.6
  89.5 19.5 %copy-start.3 = (bf16[640,128]{1,0:T(8,128)(2,1)S(1)}, bf16[640,128]{1,0:T(8,128)(2,1)}, u32[]{:S(2)}) copy-start(bf16[640,128]{1,0:T(8,128)(2,1)} %refs_17_.1) | copy-start | bytes 491524
  89.5 19.5 %copy-start.10 = (f32[128]{0:T(128)S(1)}, f32[128]{0:T(128)}, u32[]{:S(2)}) copy-start(f32[128]{0:T(128)} %param.29) | copy-start | bytes 1540
  89.5 19.5 %copy-start.11 = (f32[128]{0:T(128)S(1)}, f32[128]{0:T(128)}, u32[]{:S(2)}) copy-start(f32[128]{0:T(128)} %param.28) | copy-start | bytes 1540
  89.5 1.9 %collective-permute-start.11 = (f32[640,128]{1,0:T(8,128)}, f32[640,128]{1,0:T(8,128)S(1)}, u32[]{:S(2)}, u32[]{:S(2)}) collective-permute-start(f32[640,128]{1,0:T(8,128)} %get-tuple-element.28), channel_id=1, source_target_pairs={{0,1},{1,0},{2,3},{3,2},{4,5},{5,4},{6,7},{7,6},{8,9},{9,8},{10,11... | collective-permute-start | bytes 983048 | tf_op jit(solution)/shard_map/ppermute | solution.py:513
  89.6 3.0 %collective-permute-start.10 = (f32[640,128]{1,0:T(8,128)}, f32[640,128]{1,0:T(8,128)S(1)}, u32[]{:S(2)}, u32[]{:S(2)}) collective-permute-start(f32[640,128]{1,0:T(8,128)} %get-tuple-element.26), channel_id=1, source_target_pairs={{0,1},{1,0},{2,3},{3,2},{4,5},{5,4},{6,7},{7,6},{8,9},{9,8},{10,11... | collective-permute-start | bytes 983048 | tf_op jit(solution)/shard_map/ppermute | solution.py:515
  92.4 7.8 %collective-permute-start.12 = (bf16[640,128]{1,0:T(8,128)(2,1)S(1)}, bf16[640,128]{1,0:T(8,128)(2,1)S(1)}, u32[]{:S(2)}, u32[]{:S(2)}) collective-permute-start(bf16[640,128]{1,0:T(8,128)(2,1)S(1)} %add_convert_fusion.1), channel_id=1, source_target_pairs={{0,2},{1,3},{2,0},{3,1},{4,6},{5,7},{6,4},{7,5},{8,10},{9,11},{10,... | collective-permute-start | bytes 491528 | tf_op jit(solution)/shard_map/ppermute | solution.py:514
